TPU v7x, 256 devices: a whole 4x4x8 slice. The times are simulated.
256 devices in a mesh: row: 64 (over x, y, z_hi, core), col: 4 (over z_lo).
Axes of the slice: x: 4, y: 4, z: 8 (z_hi: 2, z_lo: 4; z = z_hi * 4 + z_lo), core: 2. Of those that a mesh axis runs over, the one named last changes fastest.
Arguments:
- sweep_start: int32 [8], replicated, may hold values from 1 to 63, as said below
- block_len: int32 [8, 256], P(None, 'row'), may hold values from 64 to 128, as said below
- reflectors: float32 [8, 256, 128, 64], P('col', 'row'), may hold values from -8 to 8, as said below
- tfactors: float32 [8, 256, 64, 64], P('col', 'row'), may hold values from -2 to 2, as said below
- panel: float32 [32768, 128], P('row'), may hold values from -180 to 180
- eigvecs: float32 [32768, 2048], P('row', 'col'), may hold values from -4 to 4
Outputs:
- result: float32 [32768, 2048], P('row', 'col')
Inputs may be any that keep to these rules, and one draw needn't show every extreme that they name: `sweep_start`: some sweep starts at row 63. In the last block of each sweep, sweep_start plus block_len is at most 128. `reflectors`: each block's vectors are unit lower trapezoidal: entry (k, k) is 1 and entries above it are 0. tfactors[s, b] is the triangular factor that makes the block a product of Householder reflections of its masked vectors.
All inputs are finite; a program needn't handle non-finite values.
Results may differ from a plain program's by a relative error of at most 0.0003.
Values sent between devices are 32-bit elements; how exact they have to be, the bound alone decides.
No kernel may reach another device: no remote copies, remote signals or barrier semaphores. Data moves between devices by JAX's collectives and lax.ppermute only.
A program may use at most 64 MiB of HBM per device.

v0:
```python
import functools

import jax
import jax.numpy as jnp
from jax import lax
from jax.experimental import pallas as pl
from jax.experimental.pallas import tpu as pltpu
from jax.sharding import PartitionSpec as P

F32 = jnp.float32
BF16 = jnp.bfloat16
BAND = 128
KREF = 64
HALF = 64
ROWS = 512
COLS = 512
ABOVE = BAND
EXT = ABOVE + ROWS + HALF
EXTRA = 2 * KREF * BAND // COLS
DOWN = BAND + EXTRA
VMEM = pl.BlockSpec(memory_space=pltpu.VMEM)
SMEM = pl.BlockSpec(memory_space=pltpu.SMEM)
PARAMS = pltpu.CompilerParams(vmem_limit_bytes=48 * 1024 * 1024)


def halves(value):
    high = value.astype(BF16)
    return high, (value - high.astype(F32)).astype(BF16)


def product(left, right):
    (lh, ll), (rh, rl) = left, right
    dot = functools.partial(jnp.dot, preferred_element_type=F32)
    return dot(lh, rh) + (dot(ll, rh) + dot(lh, rl))


def full_dot(left, right):
    return jnp.dot(left, right, precision=lax.Precision.HIGHEST, preferred_element_type=F32)


def pack_kernel(lens, reflect, factor, out):
    row = lax.broadcasted_iota(jnp.int32, (KREF, BAND), 0)
    lane = lax.broadcasted_iota(jnp.int32, (KREF, BAND), 1)
    below = jnp.zeros((BAND - KREF, KREF), F32)
    for j in range(reflect.shape[0]):
        for b in range(reflect.shape[1]):
            side = jnp.concatenate([factor[j, b], below], axis=0)
            turned = jnp.concatenate([reflect[j, b], side], axis=1).T
            live = jnp.where(lane < lens[j, b], turned[:KREF], 0.0)
            out[j, b] = jnp.where(lane > row, live, turned[KREF:])


def pack(lens, reflect, factor):
    shape = (*reflect.shape[:2], KREF, BAND)
    return pl.pallas_call(
        pack_kernel,
        out_shape=jax.ShapeDtypeStruct(shape, F32),
        in_specs=[SMEM, VMEM, VMEM],
        out_specs=VMEM,
        compiler_params=PARAMS,
        name="pack",
    )(lens, reflect, factor)


def unpacked(tile, start):
    row = lax.broadcasted_iota(jnp.int32, (KREF, BAND), 0)
    lane = lax.broadcasted_iota(jnp.int32, (KREF, BAND), 1)
    vectors = jnp.where(lane > row, tile, jnp.where(lane == row, 1.0, 0.0))
    vectors = pltpu.roll(vectors, start, 1)
    factor = jnp.where(lane <= row, tile, 0.0)[:, :KREF]
    scaled = product(halves(factor), halves(vectors))
    return [[jnp.where(part, v, 0.0) for part in (lane >= start, lane < start)] for v in (vectors, scaled)]


def apply_blocks(window, start, packed):
    ready = {j: unpacked(tile, start) for j, tile in packed.items()}
    tiles = {}
    for j in sorted({*packed, *(j + 1 for j in packed)}):
        parts = [(b, half) for half, b in enumerate((j, j - 1)) if b in packed]
        size = HALF if j not in packed else BAND
        tiles[j] = (parts, pl.ds(BAND * j, size), size)
    inner = {}
    for parts, place, size in tiles.values():
        left = jnp.concatenate([ready[b][0][half] for b, half in parts], axis=0)[:, :size]
        got = product(halves(left), halves(window[place, :]))
        for k, (b, _) in enumerate(parts):
            piece = got[k * KREF : (k + 1) * KREF]
            inner[b] = inner[b] + piece if b in inner else piece
    inner = {b: halves(value) for b, value in inner.items()}
    for parts, place, size in tiles.values():
        left = jnp.concatenate([ready[b][1][half] for b, half in parts], axis=0).T[:size]
        right = [jnp.concatenate([inner[b][k] for b, _ in parts], axis=0) for k in range(2)]
        window[place, :] = window[place, :] - product(halves(left), right)


def send_off(window, own, above, upward, downward):
    own[...] = window[ABOVE : ABOVE + ROWS, :]
    upward[...] = window[ABOVE : ABOVE + HALF, :]
    downward[:BAND, :] = window[ABOVE + ROWS - BAND : ABOVE + ROWS, :]
    step = KREF * BAND // COLS
    for k, tile in enumerate(above):
        for q in range(COLS // BAND):
            place = pl.ds(BAND + step * k, step)
            downward[place, q * BAND : (q + 1) * BAND] = tile[q * step : (q + 1) * step, :]


def received_tiles(message):
    step = KREF * BAND // COLS
    return [
        jnp.concatenate(
            [
                message[BAND + step * k : BAND + step * (k + 1), q * BAND : (q + 1) * BAND]
                for q in range(COLS // BAND)
            ],
            axis=0,
        )
        for k in range(2)
    ]


def first_kernel(starts, vectors, packed0, packed1, own, upward, downward, window):
    window[ABOVE : ABOVE + ROWS, :] = vectors[...]
    apply_blocks(window, starts[0], {b + 1: packed0[0, 0, b] for b in range(3)})
    send_off(window, own, [packed0[0, 0, 3], packed1[0, 0, 3]], upward, downward)


def join_pieces(window, vectors, from_above, from_below):
    window[:ABOVE, :] = from_above[:BAND, :]
    window[ABOVE : ABOVE + ROWS, :] = vectors[...]
    window[ABOVE + ROWS :, :] = from_below[...]


def middle_kernel(
    sweep, starts, vectors, from_above, from_below, pa, pb, pc, pd, own, upward, downward, window
):
    join_pieces(window, vectors, from_above, from_below)
    edge = received_tiles(from_above)
    apply_blocks(window, starts[sweep], {0: edge[0], 4: pa[0, 0, 3]})
    apply_blocks(
        window, starts[sweep + 1], {0: edge[1], **{b + 1: pb[0, 0, b] for b in range(4)}}
    )
    apply_blocks(window, starts[sweep + 2], {b + 1: pc[0, 0, b] for b in range(3)})
    send_off(window, own, [pc[0, 0, 3], pd[0, 0, 3]], upward, downward)


def last_kernel(
    sweep, starts, vectors, from_above, from_below, panel, pa, pb, own, partial, window
):
    join_pieces(window, vectors, from_above, from_below)
    edge = received_tiles(from_above)
    apply_blocks(window, starts[sweep], {0: edge[0], 4: pa[0, 0, 3]})
    apply_blocks(
        window, starts[sweep + 1], {0: edge[1], **{b + 1: pb[0, 0, b] for b in range(4)}}
    )
    done = window[ABOVE : ABOVE + ROWS, :]
    own[...] = done
    turned = panel[...].T
    partial[:, :COLS] = product(halves(turned), halves(done))
    partial[:, COLS:] = full_dot(turned, panel[...])


def whole(shape):
    return pl.BlockSpec(shape, lambda i: (0,) * len(shape))


def of_sweep(sweep):
    return pl.BlockSpec((1, 1, 4, KREF, BAND), lambda i: (sweep // 2, sweep % 2, 0, 0, 0))


OWN = (ROWS, COLS)
UP = (HALF, COLS)


def sent_shapes():
    return [jax.ShapeDtypeStruct(s, F32) for s in (OWN, UP, (DOWN, COLS))]


def call(kernel, out, in_specs, name):
    return pl.pallas_call(
        kernel,
        grid=(1,),
        out_shape=out,
        in_specs=in_specs,
        out_specs=[whole(o.shape) for o in out],
        scratch_shapes=[pltpu.VMEM((EXT, COLS), F32)],
        compiler_params=PARAMS,
        name=name,
    )


def first(starts, vectors, packed):
    specs = [SMEM, whole(OWN), of_sweep(0), of_sweep(1)]
    return call(first_kernel, sent_shapes(), specs, "first")(starts, vectors, packed, packed)


def middle(sweep, starts, vectors, from_above, from_below, packed):
    specs = [SMEM, whole(OWN), whole((DOWN, COLS)), whole(UP)]
    specs += [of_sweep(sweep + k) for k in range(4)]
    kernel = functools.partial(middle_kernel, sweep)
    run = call(kernel, sent_shapes(), specs, "middle")
    return run(starts, vectors, from_above, from_below, *[packed] * 4)


def last(sweep, starts, vectors, from_above, from_below, panel, packed):
    specs = [SMEM, whole(OWN), whole((DOWN, COLS)), whole(UP), whole((ROWS, BAND))]
    specs += [of_sweep(sweep + k) for k in range(2)]
    out = [jax.ShapeDtypeStruct(s, F32) for s in (OWN, (BAND, COLS + BAND))]
    kernel = functools.partial(last_kernel, sweep)
    run = call(kernel, out, specs, "last")
    return run(starts, vectors, from_above, from_below, panel, packed, packed)


def final_kernel(vectors, panel, total, out):
    row = lax.broadcasted_iota(jnp.int32, (BAND, BAND), 0)
    lane = lax.broadcasted_iota(jnp.int32, (BAND, BAND), 1)
    gram = total[:, COLS:]
    identity = jnp.where(row == lane, 1.0, 0.0)
    kept = 0.5 * gram * identity
    down = jnp.sum(kept, axis=1, keepdims=True)
    across = jnp.sum(kept, axis=0, keepdims=True)
    powered = jnp.where(lane > row, gram, 0.0) / down
    inverse = identity - powered
    reach = 1
    while reach * 2 < BAND:
        powered = full_dot(powered, powered)
        inverse = full_dot(inverse, identity + powered)
        reach = reach * 2
    inner = product(halves(inverse / across), halves(total[:, :COLS]))
    out[...] = vectors[...] - product(halves(panel[...]), halves(inner))


def final(vectors, panel, total):
    return pl.pallas_call(
        final_kernel,
        out_shape=jax.ShapeDtypeStruct(OWN, F32),
        in_specs=[VMEM] * 3,
        out_specs=VMEM,
        compiler_params=PARAMS,
        name="final",
    )(vectors, panel, total)


def shifted(value, steps):
    count = lax.axis_size("row")
    begin, end = max(0, -steps), min(count, count - steps)
    return lax.ppermute(value, "row", [(k, k + steps) for k in range(begin, end)])


def swapped(value, bit):
    return lax.ppermute(value, "row", [(k, k ^ bit) for k in range(lax.axis_size("row"))])


def spread(value, groups):
    return lax.all_to_all(
        value, "row", split_axis=0, concat_axis=0, tiled=True, axis_index_groups=groups
    )


def row_sum(value):
    count = lax.axis_size("row")
    groups = [list(range(k, count, 4)) for k in range(4)]
    size = count // 4
    core = lax.axis_index("row") % 2
    rows, width = value.shape
    half = rows // 2
    kept = lax.dynamic_slice_in_dim(value, core * half, half, 0)
    given = lax.dynamic_slice_in_dim(value, (1 - core) * half, half, 0)
    kept = kept + swapped(given, 1)
    share = spread(kept.reshape(size, half // size, width), groups).sum(axis=0)
    share = share + swapped(share, 2)
    copies = jnp.broadcast_to(share, (size, *share.shape))
    kept = spread(copies, groups).reshape(half, width)
    other = swapped(kept, 1)
    upper = jnp.where(core == 0, kept, other)
    lower = jnp.where(core == 0, other, kept)
    return jnp.concatenate([upper, lower], axis=0)


def body(sweep_start, block_len, reflectors, tfactors, panel, eigvecs):
    mine = reflectors.shape[0]
    col = lax.axis_index("col")
    lens = lax.dynamic_slice_in_dim(block_len, col * mine, mine, 0)
    packed = pack(lens, reflectors, tfactors)
    copies = jnp.broadcast_to(packed, (lax.axis_size("col"), *packed.shape))
    packed = lax.all_to_all(copies, "col", split_axis=0, concat_axis=0, tiled=True)
    sweeps = mine * lax.axis_size("col")
    vectors, upward, downward = first(sweep_start, eigvecs, packed)
    for sweep in range(0, sweeps, 2):
        from_below = shifted(upward, -1)
        from_above = shifted(downward, 1)
        pieces = (sweep_start, vectors, from_above, from_below)
        if sweep + 2 < sweeps:
            vectors, upward, downward = middle(sweep, *pieces, packed)
        else:
            vectors, partial = last(sweep, *pieces, panel, packed)
    return final(vectors, panel, row_sum(partial))


def solution(mesh):
    in_specs = (
        P(),
        P(None, "row"),
        P("col", "row", None, None),
        P("col", "row", None, None),
        P("row", None),
        P("row", "col"),
    )
    out_specs = P("row", "col")
    return jax.shard_map(body, mesh=mesh, in_specs=in_specs, out_specs=out_specs, check_vma=False)
```

profile of v0, /device:TPU:1, one launch (start us, length us, event | category | flops | bytes accessed | tf_op | source)
XLA Modules:
  0.0 169.3 jit_solution(17180223453740582860)
XLA Ops:
  0.9 1.2 copy.8.reflect
  2.1 0.8 pack.1
  3.1 31.3 %all_to_all.15.packed0.packed1.pa.pb.pc.pd = f32[4,2,4,64,128]{4,3,2,1,0:T(8,128)S(1)} all-to-all(f32[4,2,4,64,128]{4,3,2,1,0:T(8,128)S(1)} %broadcast_in_dim.6), channel_id=1, replica_groups=mesh['row'=64,'col'=4] {'col'}, dimensions={0} | all-to-all | bytes 2097152 | tf_op jit(solution)/shard_map/all_to_all | solution.py:285
  34.3 1.9 %first.1 = (f32[512,512]{1,0:T(8,128)S(1)}, f32[64,512]{1,0:T(8,128)S(1)}, f32[160,512]{1,0:T(8,128)S(1)}) custom-call(s32[8]{0:T(128)S(1)} %copy-done.7, f32[512,512]{1,0:T(8,128)S(1)} %copy-done.1, f32[4,2,4,64,128]{4,3,2,1,0:T(8,128)S(1)} %all_to_all.15.packed0.packed1.pa.pb.pc.pd, f32[4,2,4,64,128]{4,3,2,1,0:T(8,128)S(1)} %all_to_all.15.packed0.packed1.pa.pb.pc.pd), custom_call_target="tpu_custom_call" | custom-call | tf_op jit(solution)/shard_map/first/pallas_call | solution.py:193
  36.2 7.8 %collective-permute-start = (f32[160,512]{1,0:T(8,128)S(1)}, f32[160,512]{1,0:T(8,128)S(1)}, u32[]{:S(2)}, u32[]{:S(2)}) collective-permute-start(f32[160,512]{1,0:T(8,128)S(1)} %get-tuple-element.20), channel_id=1, source_target_pairs={{0,4},{4,8},{8,12},{12,16},{16,20},{20,24},{24,28},{28,32},{32,36}... | collective-permute-start | bytes 983048 | tf_op jit(solution)/shard_map/ppermute | solution.py:246
  44.0 1.9 %collective-permute-start.1 = (f32[64,512]{1,0:T(8,128)S(1)}, f32[64,512]{1,0:T(8,128)S(1)}, u32[]{:S(2)}, u32[]{:S(2)}) collective-permute-start(f32[64,512]{1,0:T(8,128)S(1)} %get-tuple-element.21), channel_id=1, source_target_pairs={{4,0},{8,4},{12,8},{16,12},{20,16},{24,20},{28,24},{32,28},{36,32}... | collective-permute-start | bytes 393224 | tf_op jit(solution)/shard_map/ppermute | solution.py:246
  45.9 9.7 %collective-permute-done.1.from_below = f32[64,512]{1,0:T(8,128)S(1)} collective-permute-done((f32[64,512]{1,0:T(8,128)S(1)}, f32[64,512]{1,0:T(8,128)S(1)}, u32[]{:S(2)}, u32[]{:S(2)}) %collective-permute-start.1) | collective-permute-done | bytes 131104 | tf_op jit(solution)/shard_map/ppermute | solution.py:246
  55.6 3.6 %middle.3 = (f32[512,512]{1,0:T(8,128)S(1)}, f32[64,512]{1,0:T(8,128)S(1)}, f32[160,512]{1,0:T(8,128)S(1)}) custom-call(s32[8]{0:T(128)S(1)} %copy-done.7, f32[512,512]{1,0:T(8,128)S(1)} %get-tuple-element.19.vectors, f32[160,512]{1,0:T(8,128)S(1)} %collective-permute-done.from_above, f32[64,512]{1,0:T(8,128)S(1)} %collective-permute-done.1.from_below, ...), custom_call_target="tpu_custom_call" | custom-call | tf_op jit(solution)/shard_map/middle/pallas_call | solution.py:201
  59.2 4.9 %collective-permute-start.2 = (f32[160,512]{1,0:T(8,128)S(1)}, f32[160,512]{1,0:T(8,128)S(1)}, u32[]{:S(2)}, u32[]{:S(2)}) collective-permute-start(f32[160,512]{1,0:T(8,128)S(1)} %get-tuple-element.23), channel_id=1, source_target_pairs={{0,4},{4,8},{8,12},{12,16},{16,20},{20,24},{24,28},{28,32},{32,36}... | collective-permute-start | bytes 983048 | tf_op jit(solution)/shard_map/ppermute | solution.py:246
  64.1 1.9 %collective-permute-start.3 = (f32[64,512]{1,0:T(8,128)S(1)}, f32[64,512]{1,0:T(8,128)S(1)}, u32[]{:S(2)}, u32[]{:S(2)}) collective-permute-start(f32[64,512]{1,0:T(8,128)S(1)} %get-tuple-element.24), channel_id=1, source_target_pairs={{4,0},{8,4},{12,8},{16,12},{20,16},{24,20},{28,24},{32,28},{36,32}... | collective-permute-start | bytes 393224 | tf_op jit(solution)/shard_map/ppermute | solution.py:246
  66.0 9.8 %collective-permute-done.3.from_below = f32[64,512]{1,0:T(8,128)S(1)} collective-permute-done((f32[64,512]{1,0:T(8,128)S(1)}, f32[64,512]{1,0:T(8,128)S(1)}, u32[]{:S(2)}, u32[]{:S(2)}) %collective-permute-start.3) | collective-permute-done | bytes 131104 | tf_op jit(solution)/shard_map/ppermute | solution.py:246
  75.8 3.6 %middle.4 = (f32[512,512]{1,0:T(8,128)S(1)}, f32[64,512]{1,0:T(8,128)S(1)}, f32[160,512]{1,0:T(8,128)S(1)}) custom-call(s32[8]{0:T(128)S(1)} %copy-done.7, f32[512,512]{1,0:T(8,128)S(1)} %get-tuple-element.22.vectors, f32[160,512]{1,0:T(8,128)S(1)} %collective-permute-done.2.from_above, f32[64,512]{1,0:T(8,128)S(1)} %collective-permute-done.3.from_below, ...), custom_call_target="tpu_custom_call" | custom-call | tf_op jit(solution)/shard_map/middle/pallas_call | solution.py:201
  79.4 3.3 %collective-permute-start.4 = (f32[160,512]{1,0:T(8,128)S(1)}, f32[160,512]{1,0:T(8,128)S(1)}, u32[]{:S(2)}, u32[]{:S(2)}) collective-permute-start(f32[160,512]{1,0:T(8,128)S(1)} %get-tuple-element.26), channel_id=1, source_target_pairs={{0,4},{4,8},{8,12},{12,16},{16,20},{20,24},{24,28},{28,32},{32,36}... | collective-permute-start | bytes 983048 | tf_op jit(solution)/shard_map/ppermute | solution.py:246
  82.7 1.9 %collective-permute-start.5 = (f32[64,512]{1,0:T(8,128)S(1)}, f32[64,512]{1,0:T(8,128)S(1)}, u32[]{:S(2)}, u32[]{:S(2)}) collective-permute-start(f32[64,512]{1,0:T(8,128)S(1)} %get-tuple-element.27), channel_id=1, source_target_pairs={{4,0},{8,4},{12,8},{16,12},{20,16},{24,20},{28,24},{32,28},{36,32}... | collective-permute-start | bytes 393224 | tf_op jit(solution)/shard_map/ppermute | solution.py:246
  84.7 11.8 %collective-permute-done.5.from_below = f32[64,512]{1,0:T(8,128)S(1)} collective-permute-done((f32[64,512]{1,0:T(8,128)S(1)}, f32[64,512]{1,0:T(8,128)S(1)}, u32[]{:S(2)}, u32[]{:S(2)}) %collective-permute-start.5) | collective-permute-done | bytes 131104 | tf_op jit(solution)/shard_map/ppermute | solution.py:246
  96.5 4.3 %middle.5 = (f32[512,512]{1,0:T(8,128)S(1)}, f32[64,512]{1,0:T(8,128)}, f32[160,512]{1,0:T(8,128)}) custom-call(s32[8]{0:T(128)S(1)} %copy-done.7, f32[512,512]{1,0:T(8,128)S(1)} %get-tuple-element.25.vectors, f32[160,512]{1,0:T(8,128)S(1)} %collective-permute-done.4.from_above, f32[64,512]{1,0:T(8,128)S(1)} %collective-permute-done.5.from_below, ...), custom_call_target="tpu_custom_call" | custom-call | tf_op jit(solution)/shard_map/middle/pallas_call | solution.py:201
  100.8 1.9 %collective-permute-start.6 = (f32[160,512]{1,0:T(8,128)}, f32[160,512]{1,0:T(8,128)S(1)}, u32[]{:S(2)}, u32[]{:S(2)}) collective-permute-start(f32[160,512]{1,0:T(8,128)} %get-tuple-element.29), channel_id=1, source_target_pairs={{0,4},{4,8},{8,12},{12,16},{16,20},{20,24},{24,28},{28,32},{32,36}... | collective-permute-start | bytes 983048 | tf_op jit(solution)/shard_map/ppermute | solution.py:246
  102.7 2.6 %collective-permute-start.7 = (f32[64,512]{1,0:T(8,128)}, f32[64,512]{1,0:T(8,128)S(1)}, u32[]{:S(2)}, u32[]{:S(2)}) collective-permute-start(f32[64,512]{1,0:T(8,128)} %get-tuple-element.30), channel_id=1, source_target_pairs={{4,0},{8,4},{12,8},{16,12},{20,16},{24,20},{28,24},{32,28},{36,32}... | collective-permute-start | bytes 393224 | tf_op jit(solution)/shard_map/ppermute | solution.py:246
  105.3 12.4 %collective-permute-done.7.from_below = f32[64,512]{1,0:T(8,128)S(1)} collective-permute-done((f32[64,512]{1,0:T(8,128)}, f32[64,512]{1,0:T(8,128)S(1)}, u32[]{:S(2)}, u32[]{:S(2)}) %collective-permute-start.7) | collective-permute-done | bytes 131104 | tf_op jit(solution)/shard_map/ppermute | solution.py:246
  117.7 0.7 copy-done.3
  118.4 1.0 copy-done.4
  119.4 3.4 %last.1 = (f32[512,512]{1,0:T(8,128)S(1)}, f32[128,640]{1,0:T(8,128)S(1)}) custom-call(s32[8]{0:T(128)S(1)} %copy-done.7, f32[512,512]{1,0:T(8,128)S(1)} %get-tuple-element.28.vectors, f32[160,512]{1,0:T(8,128)S(1)} %copy-done.4, f32[64,512]{1,0:T(8,128)S(1)} %collective-permute-done.7.from_below, f32[512,128]{1,0:T(8,128)S(1)} %copy-done.2, ...), custom_call_target="tpu_custom_call" | custom-call | tf_op jit(solution)/shard_map/last/pallas_call | solution.py:210
  122.8 0.7 copy-done.5
  123.6 1.4 collective-permute-done.8
  125.0 0.9 dynamic-slice_add_fusion
  126.0 16.2 %all_to_all.16 = f32[16,4,640]{2,1,0:T(4,128)S(1)} all-to-all(f32[16,4,640]{2,1,0:T(4,128)S(1)} %reshape.6), channel_id=1, replica_groups={{0,16,32,48,64,80,96,112,128,144,160,176,192,208,224,240},{4,20,36,52,6..., dimensions={0} | all-to-all | bytes 327680 | tf_op jit(solution)/shard_map/all_to_all | solution.py:254
  142.3 7.4 %collective-permute-start.9 = (f32[4,640]{1,0:T(4,128)S(1)}, f32[4,640]{1,0:T(4,128)S(1)}, u32[]{:S(2)}, u32[]{:S(2)}) collective-permute-start(f32[4,640]{1,0:T(4,128)S(1)} %reduce_sum.9), channel_id=1, source_target_pairs={{0,8},{4,12},{8,0},{12,4},{16,24},{20,28},{24,16},{28,20},{32,40},... | collective-permute-start | bytes 30728 | tf_op jit(solution)/shard_map/ppermute | solution.py:250
  149.7 1.1 collective-permute-done.9
  150.8 10.2 %all_to_all.17 = f32[16,4,640]{2,1,0:T(4,128)S(1)} all-to-all(f32[16,4,640]{2,1,0:T(4,128)S(1)} %broadcast_in_dim.7), channel_id=1, replica_groups={{0,16,32,48,64,80,96,112,128,144,160,176,192,208,224,240},{4,20,36,52,6..., dimensions={0} | all-to-all | bytes 327680 | tf_op jit(solution)/shard_map/all_to_all | solution.py:254
  161.1 3.6 %collective-permute-start.10 = (f32[64,640]{1,0:T(8,128)S(1)}, f32[64,640]{1,0:T(8,128)S(1)}, u32[]{:S(2)}, u32[]{:S(2)}) collective-permute-start(f32[64,640]{1,0:T(8,128)S(1)} %reshape.7), channel_id=1, source_target_pairs={{0,4},{4,0},{8,12},{12,8},{16,20},{20,16},{24,28},{28,24},{32,36},... | collective-permute-start | bytes 491528 | tf_op jit(solution)/shard_map/ppermute | solution.py:250
  164.7 1.0 collective-permute-done.10
  165.8 3.5 %final.1 = f32[512,512]{1,0:T(8,128)} custom-call(f32[512,512]{1,0:T(8,128)S(1)} %get-tuple-element.31.vectors, f32[512,128]{1,0:T(8,128)S(1)} %copy-done.2, f32[128,640]{1,0:T(8,128)S(1)} %pad_maximum_fusion.total), custom_call_target="tpu_custom_call" | custom-call | tf_op jit(solution)/shard_map/final/pallas_call | solution.py:233
  (29 shorter events, 1.3 us)
Async XLA Ops:
  0.0 0.7 copy-start
  0.9 1.2 copy-start.6
  3.0 31.3 %copy-start.1 = (f32[512,512]{1,0:T(8,128)S(1)}, f32[512,512]{1,0:T(8,128)}, u32[]{:S(2)}) copy-start(f32[512,512]{1,0:T(8,128)} %vectors.1) | copy-start | bytes 3145732
  3.0 31.3 %copy-start.7 = (s32[8]{0:T(128)S(1)}, s32[8]{0:T(128)}, u32[]{:S(2)}) copy-start(s32[8]{0:T(128)} %starts.9) | copy-start | bytes 100
  36.2 19.4 %collective-permute-start = (f32[160,512]{1,0:T(8,128)S(1)}, f32[160,512]{1,0:T(8,128)S(1)}, u32[]{:S(2)}, u32[]{:S(2)}) collective-permute-start(f32[160,512]{1,0:T(8,128)S(1)} %get-tuple-element.20), channel_id=1, source_target_pairs={{0,4},{4,8},{8,12},{12,16},{16,20},{20,24},{24,28},{28,32},{32,36}... | collective-permute-start | bytes 983048 | tf_op jit(solution)/shard_map/ppermute | solution.py:246
  44.0 11.6 %collective-permute-start.1 = (f32[64,512]{1,0:T(8,128)S(1)}, f32[64,512]{1,0:T(8,128)S(1)}, u32[]{:S(2)}, u32[]{:S(2)}) collective-permute-start(f32[64,512]{1,0:T(8,128)S(1)} %get-tuple-element.21), channel_id=1, source_target_pairs={{4,0},{8,4},{12,8},{16,12},{20,16},{24,20},{28,24},{32,28},{36,32}... | collective-permute-start | bytes 393224 | tf_op jit(solution)/shard_map/ppermute | solution.py:246
  59.2 16.6 %collective-permute-start.2 = (f32[160,512]{1,0:T(8,128)S(1)}, f32[160,512]{1,0:T(8,128)S(1)}, u32[]{:S(2)}, u32[]{:S(2)}) collective-permute-start(f32[160,512]{1,0:T(8,128)S(1)} %get-tuple-element.23), channel_id=1, source_target_pairs={{0,4},{4,8},{8,12},{12,16},{16,20},{20,24},{24,28},{28,32},{32,36}... | collective-permute-start | bytes 983048 | tf_op jit(solution)/shard_map/ppermute | solution.py:246
  64.1 11.7 %collective-permute-start.3 = (f32[64,512]{1,0:T(8,128)S(1)}, f32[64,512]{1,0:T(8,128)S(1)}, u32[]{:S(2)}, u32[]{:S(2)}) collective-permute-start(f32[64,512]{1,0:T(8,128)S(1)} %get-tuple-element.24), channel_id=1, source_target_pairs={{4,0},{8,4},{12,8},{16,12},{20,16},{24,20},{28,24},{32,28},{36,32}... | collective-permute-start | bytes 393224 | tf_op jit(solution)/shard_map/ppermute | solution.py:246
  79.4 17.0 %collective-permute-start.4 = (f32[160,512]{1,0:T(8,128)S(1)}, f32[160,512]{1,0:T(8,128)S(1)}, u32[]{:S(2)}, u32[]{:S(2)}) collective-permute-start(f32[160,512]{1,0:T(8,128)S(1)} %get-tuple-element.26), channel_id=1, source_target_pairs={{0,4},{4,8},{8,12},{12,16},{16,20},{20,24},{24,28},{28,32},{32,36}... | collective-permute-start | bytes 983048 | tf_op jit(solution)/shard_map/ppermute | solution.py:246
  82.7 13.7 %collective-permute-start.5 = (f32[64,512]{1,0:T(8,128)S(1)}, f32[64,512]{1,0:T(8,128)S(1)}, u32[]{:S(2)}, u32[]{:S(2)}) collective-permute-start(f32[64,512]{1,0:T(8,128)S(1)} %get-tuple-element.27), channel_id=1, source_target_pairs={{4,0},{8,4},{12,8},{16,12},{20,16},{24,20},{28,24},{32,28},{36,32}... | collective-permute-start | bytes 393224 | tf_op jit(solution)/shard_map/ppermute | solution.py:246
  96.5 22.0 %copy-start.2 = (f32[512,128]{1,0:T(8,128)S(1)}, f32[512,128]{1,0:T(8,128)}, u32[]{:S(2)}) copy-start(f32[512,128]{1,0:T(8,128)} %panel.3) | copy-start | bytes 786436
  100.8 16.9 %collective-permute-start.6 = (f32[160,512]{1,0:T(8,128)}, f32[160,512]{1,0:T(8,128)S(1)}, u32[]{:S(2)}, u32[]{:S(2)}) collective-permute-start(f32[160,512]{1,0:T(8,128)} %get-tuple-element.29), channel_id=1, source_target_pairs={{0,4},{4,8},{8,12},{12,16},{16,20},{20,24},{24,28},{28,32},{32,36}... | collective-permute-start | bytes 983048 | tf_op jit(solution)/shard_map/ppermute | solution.py:246
  102.7 15.0 %collective-permute-start.7 = (f32[64,512]{1,0:T(8,128)}, f32[64,512]{1,0:T(8,128)S(1)}, u32[]{:S(2)}, u32[]{:S(2)}) collective-permute-start(f32[64,512]{1,0:T(8,128)} %get-tuple-element.30), channel_id=1, source_target_pairs={{4,0},{8,4},{12,8},{16,12},{20,16},{24,20},{28,24},{32,28},{36,32}... | collective-permute-start | bytes 393224 | tf_op jit(solution)/shard_map/ppermute | solution.py:246
  117.7 0.7 copy-start.3
  118.4 1.0 copy-start.4
  122.8 0.7 copy-start.5
  123.5 1.5 collective-permute-start.8
  142.3 8.5 %collective-permute-start.9 = (f32[4,640]{1,0:T(4,128)S(1)}, f32[4,640]{1,0:T(4,128)S(1)}, u32[]{:S(2)}, u32[]{:S(2)}) collective-permute-start(f32[4,640]{1,0:T(4,128)S(1)} %reduce_sum.9), channel_id=1, source_target_pairs={{0,8},{4,12},{8,0},{12,4},{16,24},{20,28},{24,16},{28,20},{32,40},... | collective-permute-start | bytes 30728 | tf_op jit(solution)/shard_map/ppermute | solution.py:250
  161.1 4.7 %collective-permute-start.10 = (f32[64,640]{1,0:T(8,128)S(1)}, f32[64,640]{1,0:T(8,128)S(1)}, u32[]{:S(2)}, u32[]{:S(2)}) collective-permute-start(f32[64,640]{1,0:T(8,128)S(1)} %reshape.7), channel_id=1, source_target_pairs={{0,4},{4,0},{8,12},{12,8},{16,20},{20,16},{24,28},{28,24},{32,36},... | collective-permute-start | bytes 491528 | tf_op jit(solution)/shard_map/ppermute | solution.py:250
where the time goes:
time: 170 us; the launch traced here: 169 us
  blocking collectives  57.7 us (34%)
  waiting for transfers between devices  47.1 us (28%)
  starting transfers between devices  37.3 us (22%)
  Pallas kernels  21.1 us (12%)
  local copies, waits for them, and re-layouts  4.73 us (3%)
    ppermute x8, waiting for transfers between devices, shifted(): lax.ppermute(value, 'row', [(k, k + steps) for k in range(begin, end)])  43.6 us
    all_to_all x1, blocking collectives, body(): lax.all_to_all(copies, 'col', split_axis=0, concat_axis=0, tiled=True)  31.3 us
    all_to_all x2, blocking collectives, spread(): lax.all_to_all(value, 'row', split_axis=0, concat_axis=0, tiled=True, axi...  26.4 us
    ppermute x8, starting transfers between devices, shifted(): lax.ppermute(value, 'row', [(k, k + steps) for k in range(begin, end)])  26.2 us
    pallas_call x3, Pallas kernels, middle(): return run(starts, vectors, from_above, from_below, *[packed] * 4)  11.5 us
    ppermute x3, starting transfers between devices, swapped(): lax.ppermute(value, 'row', [(k, k ^ bit) for k in range(lax.axis_size('ro...  11.1 us
    unnamed x18, local copies, waits for them, and re-layouts  4.41 us
    pallas_call x1, Pallas kernels, final(): pl.pallas_call(final_kernel, out_shape=jax.ShapeDtypeStruct(OWN, F32), in...  3.49 us
  transfers between devices with their start and end apart: 11, of which 7 were waited for; matrix products, arithmetic and copies ran while one was open for 0% of the time, Pallas kernels for 0%

commit v1 on v0

--- a/solution.py
+++ b/solution.py
@@ -16,11 +16,9 @@
 COLS = 512
 ABOVE = BAND
 EXT = ABOVE + ROWS + HALF
-EXTRA = 2 * KREF * BAND // COLS
-DOWN = BAND + EXTRA
 VMEM = pl.BlockSpec(memory_space=pltpu.VMEM)
 SMEM = pl.BlockSpec(memory_space=pltpu.SMEM)
-PARAMS = pltpu.CompilerParams(vmem_limit_bytes=48 * 1024 * 1024)
+PARAMS = pltpu.CompilerParams(vmem_limit_bytes=20 * 1024 * 1024)
 
 
 def halves(value):
@@ -62,18 +60,19 @@
     )(lens, reflect, factor)
 
 
-def unpacked(tile, start):
+def unpacked(tile, start, back):
     row = lax.broadcasted_iota(jnp.int32, (KREF, BAND), 0)
     lane = lax.broadcasted_iota(jnp.int32, (KREF, BAND), 1)
     vectors = jnp.where(lane > row, tile, jnp.where(lane == row, 1.0, 0.0))
     vectors = pltpu.roll(vectors, start, 1)
-    factor = jnp.where(lane <= row, tile, 0.0)[:, :KREF]
+    factor = jnp.where(lane <= row, tile, 0.0)
+    factor = factor.T[:KREF] if back else factor[:, :KREF]
     scaled = product(halves(factor), halves(vectors))
     return [[jnp.where(part, v, 0.0) for part in (lane >= start, lane < start)] for v in (vectors, scaled)]
 
 
-def apply_blocks(window, start, packed):
-    ready = {j: unpacked(tile, start) for j, tile in packed.items()}
+def apply_blocks(window, start, packed, back=False):
+    ready = {j: unpacked(tile, start, back) for j, tile in packed.items()}
     tiles = {}
     for j in sorted({*packed, *(j + 1 for j in packed)}):
         parts = [(b, half) for half, b in enumerate((j, j - 1)) if b in packed]
@@ -93,70 +92,117 @@
         window[place, :] = window[place, :] - product(halves(left), right)
 
 
-def send_off(window, own, above, upward, downward):
-    own[...] = window[ABOVE : ABOVE + ROWS, :]
-    upward[...] = window[ABOVE : ABOVE + HALF, :]
-    downward[:BAND, :] = window[ABOVE + ROWS - BAND : ABOVE + ROWS, :]
-    step = KREF * BAND // COLS
-    for k, tile in enumerate(above):
-        for q in range(COLS // BAND):
-            place = pl.ds(BAND + step * k, step)
-            downward[place, q * BAND : (q + 1) * BAND] = tile[q * step : (q + 1) * step, :]
-
-
-def received_tiles(message):
-    step = KREF * BAND // COLS
-    return [
-        jnp.concatenate(
-            [
-                message[BAND + step * k : BAND + step * (k + 1), q * BAND : (q + 1) * BAND]
-                for q in range(COLS // BAND)
-            ],
-            axis=0,
-        )
-        for k in range(2)
-    ]
-
-
-def first_kernel(starts, vectors, packed0, packed1, own, upward, downward, window):
-    window[ABOVE : ABOVE + ROWS, :] = vectors[...]
-    apply_blocks(window, starts[0], {b + 1: packed0[0, 0, b] for b in range(3)})
-    send_off(window, own, [packed0[0, 0, 3], packed1[0, 0, 3]], upward, downward)
-
-
-def join_pieces(window, vectors, from_above, from_below):
-    window[:ABOVE, :] = from_above[:BAND, :]
-    window[ABOVE : ABOVE + ROWS, :] = vectors[...]
-    window[ABOVE + ROWS :, :] = from_below[...]
+def slabs(width, tiles):
+    across = width // BAND
+    for n in range(tiles * KREF // 8):
+        yield n // (KREF // 8), n % (KREF // 8) * 8, BAND + n // across * 8, n % across * BAND
+
+
+def message_rows(width, tiles):
+    return BAND + -(-tiles * KREF // 8 // (width // BAND)) * 8
+
+
+def send_off(windows, upward, downward, tiles):
+    left = 0
+    for window in windows:
+        columns = pl.ds(left, window.shape[1])
+        upward[:, columns] = window[ABOVE : ABOVE + HALF, :]
+        downward[:BAND, columns] = window[ABOVE + ROWS - BAND : ABOVE + ROWS, :]
+        left += window.shape[1]
+    for k, low, row, lane in slabs(left, len(tiles)):
+        downward[row : row + 8, lane : lane + BAND] = tiles[k][low : low + 8, :]
+
+
+def join_pieces(windows, owns, from_above, from_below):
+    left = 0
+    for window, own in zip(windows, owns):
+        columns = pl.ds(left, window.shape[1])
+        window[:ABOVE, :] = from_above[:BAND, columns]
+        window[ABOVE : ABOVE + ROWS, :] = own[...]
+        window[ABOVE + ROWS :, :] = from_below[:, columns]
+        left += window.shape[1]
+    tiles = [[] for _ in range(2 * len(windows))]
+    for k, _, row, lane in slabs(left, len(tiles)):
+        tiles[k].append(from_above[row : row + 8, lane : lane + BAND])
+    return [jnp.concatenate(parts, axis=0) for parts in tiles]
+
+
+def inner(packed):
+    return {b + 1: packed[0, 0, b] for b in range(3)}
+
+
+def outer(above, packed):
+    return {0: above, 4: packed[0, 0, 3]}
+
+
+def every(above, packed):
+    return {0: above, **{b + 1: packed[0, 0, b] for b in range(4)}}
+
+
+def two_sweeps(window, starts, sweeps, edge, packed, back=False):
+    apply_blocks(window, starts[sweeps[0]], outer(edge[0], packed[0]), back)
+    apply_blocks(window, starts[sweeps[1]], every(edge[1], packed[1]), back)
+
+
+def first_kernel(
+    last_sweep, starts, vectors, panel, p0, p1, q0, q1, own, reduced, upward, downward, wide, narrow
+):
+    wide[ABOVE : ABOVE + ROWS, :] = vectors[...]
+    narrow[ABOVE : ABOVE + ROWS, :] = panel[...]
+    apply_blocks(wide, starts[0], inner(p0))
+    apply_blocks(narrow, starts[last_sweep], inner(q0), True)
+    send_off((wide, narrow), upward, downward, [p[0, 0, 3] for p in (p0, p1, q0, q1)])
+    own[...] = wide[ABOVE : ABOVE + ROWS, :]
+    reduced[...] = narrow[ABOVE : ABOVE + ROWS, :]
+
+
+def second_kernel(
+    last_sweep, starts, vectors, panel, above, below, p0, p1, p2, p3, q0, q1, q2, q3,
+    own, reduced, upward, downward, wide, narrow,
+):
+    edge = join_pieces((wide, narrow), (vectors, panel), above, below)
+    two_sweeps(wide, starts, (0, 1), edge[:2], (p0, p1))
+    two_sweeps(narrow, starts, (last_sweep, last_sweep - 1), edge[2:], (q0, q1), True)
+    apply_blocks(wide, starts[2], inner(p2))
+    apply_blocks(narrow, starts[last_sweep - 2], inner(q2), True)
+    send_off((wide, narrow), upward, downward, [p[0, 0, 3] for p in (p2, p3, q2, q3)])
+    own[...] = wide[ABOVE : ABOVE + ROWS, :]
+    reduced[...] = narrow[ABOVE : ABOVE + ROWS, :]
+
+
+def third_kernel(
+    last_sweep, starts, vectors, panel, above, below, p0, p1, p2, p3, q0, q1,
+    own, between, reduced, upward, downward, wide, narrow,
+):
+    edge = join_pieces((wide, narrow), (vectors, panel), above, below)
+    two_sweeps(wide, starts, (2, 3), edge[:2], (p0, p1))
+    two_sweeps(narrow, starts, (last_sweep - 2, last_sweep - 3), edge[2:], (q0, q1), True)
+    between[...] = wide[ABOVE : ABOVE + ROWS, :]
+    reduced[...] = narrow[ABOVE : ABOVE + ROWS, :]
+    apply_blocks(wide, starts[4], inner(p2))
+    send_off((wide,), upward, downward, [p[0, 0, 3] for p in (p2, p3)])
+    own[...] = wide[ABOVE : ABOVE + ROWS, :]
 
 
 def middle_kernel(
-    sweep, starts, vectors, from_above, from_below, pa, pb, pc, pd, own, upward, downward, window
+    sweep, starts, vectors, above, below, p0, p1, p2, p3, own, upward, downward, wide
 ):
-    join_pieces(window, vectors, from_above, from_below)
-    edge = received_tiles(from_above)
-    apply_blocks(window, starts[sweep], {0: edge[0], 4: pa[0, 0, 3]})
-    apply_blocks(
-        window, starts[sweep + 1], {0: edge[1], **{b + 1: pb[0, 0, b] for b in range(4)}}
-    )
-    apply_blocks(window, starts[sweep + 2], {b + 1: pc[0, 0, b] for b in range(3)})
-    send_off(window, own, [pc[0, 0, 3], pd[0, 0, 3]], upward, downward)
-
-
-def last_kernel(
-    sweep, starts, vectors, from_above, from_below, panel, pa, pb, own, partial, window
-):
-    join_pieces(window, vectors, from_above, from_below)
-    edge = received_tiles(from_above)
-    apply_blocks(window, starts[sweep], {0: edge[0], 4: pa[0, 0, 3]})
-    apply_blocks(
-        window, starts[sweep + 1], {0: edge[1], **{b + 1: pb[0, 0, b] for b in range(4)}}
-    )
-    done = window[ABOVE : ABOVE + ROWS, :]
-    own[...] = done
-    turned = panel[...].T
-    partial[:, :COLS] = product(halves(turned), halves(done))
-    partial[:, COLS:] = full_dot(turned, panel[...])
+    edge = join_pieces((wide,), (vectors,), above, below)
+    two_sweeps(wide, starts, (sweep, sweep + 1), edge, (p0, p1))
+    apply_blocks(wide, starts[sweep + 2], inner(p2))
+    send_off((wide,), upward, downward, [p[0, 0, 3] for p in (p2, p3)])
+    own[...] = wide[ABOVE : ABOVE + ROWS, :]
+
+
+def last_kernel(sweep, starts, vectors, above, below, p0, p1, own, wide):
+    edge = join_pieces((wide,), (vectors,), above, below)
+    two_sweeps(wide, starts, (sweep, sweep + 1), edge, (p0, p1))
+    own[...] = wide[ABOVE : ABOVE + ROWS, :]
+
+
+def project_kernel(panel, reduced, vectors, partial):
+    partial[:, :COLS] = product(halves(reduced[...].T), halves(vectors[...]))
+    partial[:, COLS:] = full_dot(panel[...].T, panel[...])
 
 
 def whole(shape):
@@ -168,46 +214,36 @@
 
 
 OWN = (ROWS, COLS)
-UP = (HALF, COLS)
-
-
-def sent_shapes():
-    return [jax.ShapeDtypeStruct(s, F32) for s in (OWN, UP, (DOWN, COLS))]
-
-
-def call(kernel, out, in_specs, name):
-    return pl.pallas_call(
+THIN = (ROWS, BAND)
+
+
+def sent(width, tiles):
+    return [(HALF, width), (message_rows(width, tiles), width)]
+
+
+def call(kernel, out, operands, packed, sweeps, widths):
+    specs = [SMEM] + [whole(o.shape) for o in operands[1:]] + [of_sweep(s) for s in sweeps]
+    run = pl.pallas_call(
         kernel,
         grid=(1,),
-        out_shape=out,
-        in_specs=in_specs,
-        out_specs=[whole(o.shape) for o in out],
-        scratch_shapes=[pltpu.VMEM((EXT, COLS), F32)],
+        out_shape=[jax.ShapeDtypeStruct(s, F32) for s in out],
+        in_specs=specs,
+        out_specs=[whole(s) for s in out],
+        scratch_shapes=[pltpu.VMEM((EXT, w), F32) for w in widths],
         compiler_params=PARAMS,
-        name=name,
-    )
-
-
-def first(starts, vectors, packed):
-    specs = [SMEM, whole(OWN), of_sweep(0), of_sweep(1)]
-    return call(first_kernel, sent_shapes(), specs, "first")(starts, vectors, packed, packed)
-
-
-def middle(sweep, starts, vectors, from_above, from_below, packed):
-    specs = [SMEM, whole(OWN), whole((DOWN, COLS)), whole(UP)]
-    specs += [of_sweep(sweep + k) for k in range(4)]
-    kernel = functools.partial(middle_kernel, sweep)
-    run = call(kernel, sent_shapes(), specs, "middle")
-    return run(starts, vectors, from_above, from_below, *[packed] * 4)
-
-
-def last(sweep, starts, vectors, from_above, from_below, panel, packed):
-    specs = [SMEM, whole(OWN), whole((DOWN, COLS)), whole(UP), whole((ROWS, BAND))]
-    specs += [of_sweep(sweep + k) for k in range(2)]
-    out = [jax.ShapeDtypeStruct(s, F32) for s in (OWN, (BAND, COLS + BAND))]
-    kernel = functools.partial(last_kernel, sweep)
-    run = call(kernel, out, specs, "last")
-    return run(starts, vectors, from_above, from_below, panel, packed, packed)
+    )
+    return run(*operands, *[packed] * len(sweeps))
+
+
+def project(panel, reduced, vectors):
+    return pl.pallas_call(
+        project_kernel,
+        out_shape=jax.ShapeDtypeStruct((BAND, COLS + BAND), F32),
+        in_specs=[VMEM] * 3,
+        out_specs=VMEM,
+        compiler_params=PARAMS,
+        name="project",
+    )(panel, reduced, vectors)
 
 
 def final_kernel(vectors, panel, total, out):
@@ -283,17 +319,38 @@
     packed = pack(lens, reflectors, tfactors)
     copies = jnp.broadcast_to(packed, (lax.axis_size("col"), *packed.shape))
     packed = lax.all_to_all(copies, "col", split_axis=0, concat_axis=0, tiled=True)
-    sweeps = mine * lax.axis_size("col")
-    vectors, upward, downward = first(sweep_start, eigvecs, packed)
-    for sweep in range(0, sweeps, 2):
-        from_below = shifted(upward, -1)
-        from_above = shifted(downward, 1)
-        pieces = (sweep_start, vectors, from_above, from_below)
-        if sweep + 2 < sweeps:
-            vectors, upward, downward = middle(sweep, *pieces, packed)
-        else:
-            vectors, partial = last(sweep, *pieces, panel, packed)
-    return final(vectors, panel, row_sum(partial))
+    end = mine * lax.axis_size("col") - 1
+    both = (COLS, BAND)
+    wide = COLS + BAND
+
+    def exchanged(upward, downward):
+        above = shifted(downward, 1)
+        return above, shifted(upward, -1)
+
+    vectors, reduced, upward, downward = call(
+        functools.partial(first_kernel, end), [OWN, THIN, *sent(wide, 4)],
+        (sweep_start, eigvecs, panel), packed, (0, 1, end, end - 1), both,
+    )
+    vectors, reduced, upward, downward = call(
+        functools.partial(second_kernel, end), [OWN, THIN, *sent(wide, 4)],
+        (sweep_start, vectors, reduced, *exchanged(upward, downward)), packed,
+        (0, 1, 2, 3, end, end - 1, end - 2, end - 3), both,
+    )
+    vectors, between, reduced, upward, downward = call(
+        functools.partial(third_kernel, end), [OWN, OWN, THIN, *sent(COLS, 2)],
+        (sweep_start, vectors, reduced, *exchanged(upward, downward)), packed,
+        (2, 3, 4, 5, end - 2, end - 3), both,
+    )
+    total = row_sum(project(panel, reduced, between))
+    vectors, upward, downward = call(
+        functools.partial(middle_kernel, 4), [OWN, *sent(COLS, 2)],
+        (sweep_start, vectors, *exchanged(upward, downward)), packed, (4, 5, 6, 7), (COLS,),
+    )
+    (vectors,) = call(
+        functools.partial(last_kernel, 6), [OWN],
+        (sweep_start, vectors, *exchanged(upward, downward)), packed, (6, 7), (COLS,),
+    )
+    return final(vectors, panel, total)
 
 
 def solution(mesh):

time: 170 us -> 177 us (1.041)
  the two profiles are of different devices: /device:TPU:1 before, /device:TPU:34 now
where the time goes in v1:
time: 177 us; the launch traced here: 176 us
  starting transfers between devices  62 us (35%)
  blocking collectives  43.9 us (25%)
  waiting for transfers between devices  36 us (20%)
  Pallas kernels  24.8 us (14%)
  local copies, waits for them, and re-layouts  8.11 us (5%)
    ppermute x8, starting transfers between devices, shifted(): lax.ppermute(value, 'row', [(k, k + steps) for k in range(begin, end)])  47.8 us
    all_to_all x1, blocking collectives, body(): lax.all_to_all(copies, 'col', split_axis=0, concat_axis=0, tiled=True)  29.8 us
    ppermute x8, waiting for transfers between devices, shifted(): lax.ppermute(value, 'row', [(k, k + steps) for k in range(begin, end)])  28.1 us
    pallas_call x5, Pallas kernels, call(): return run(*operands, *[packed] * len(sweeps))  19.8 us
    all_to_all x1, blocking collectives, spread(): lax.all_to_all(value, 'row', split_axis=0, concat_axis=0, tiled=True, axi...  14 us
    ppermute x3, starting transfers between devices, swapped(): lax.ppermute(value, 'row', [(k, k ^ bit) for k in range(lax.axis_size('ro...  9.3 us
    unnamed x28, local copies, waits for them, and re-layouts  7.11 us
    all_to_all x1, starting transfers between devices, spread(): lax.all_to_all(value, 'row', split_axis=0, concat_axis=0, tiled=True, axi...  4.86 us
  transfers between devices with their start and end apart: 12, of which 9 were waited for; matrix products, arithmetic and copies ran while one was open for 1% of the time, Pallas kernels for 2%

profile of v1, /device:TPU:34, one launch (start us, length us, event | category | flops | bytes accessed | tf_op | source)
XLA Modules:
  0.0 176.0 jit_solution(640941963468890927)
XLA Ops:
  0.9 1.2 copy.8.reflect
  3.1 29.8 %all_to_all.15.p0.p1.q0.q1.p2.p3.q2.q3 = f32[4,2,4,64,128]{4,3,2,1,0:T(8,128)S(1)} all-to-all(f32[4,2,4,64,128]{4,3,2,1,0:T(8,128)S(1)} %broadcast_in_dim.6), channel_id=1, replica_groups=mesh['row'=64,'col'=4] {'col'}, dimensions={0} | all-to-all | bytes 2097152 | tf_op jit(solution)/shard_map/all_to_all | solution.py:321
  32.9 2.3 %shard_map.64 = (f32[512,512]{1,0:T(8,128)S(1)}, f32[512,128]{1,0:T(8,128)S(1)}, f32[64,640]{1,0:T(8,128)S(1)}, f32[184,640]{1,0:T(8,128)S(1)}) custom-call(s32[8]{0:T(128)S(1)} %copy-done.10, f32[512,512]{1,0:T(8,128)S(1)} %copy-done.2, f32[512,128]{1,0:T(8,128)S(1)} %copy-done.1, f32[4,2,4,64,128]{4,3,2,1,0:T(8,128)S(1)} %all_to_all.15.p0.p1.q0.q1.p2.p3.q2.q3, ...), custom_call_target="tpu_custom_call" | custom-call | tf_op jit(solution)/shard_map/pallas_call | solution.py:235
  35.2 1.9 %collective-permute-start = (f32[184,640]{1,0:T(8,128)S(1)}, f32[184,640]{1,0:T(8,128)S(1)}, u32[]{:S(2)}, u32[]{:S(2)}) collective-permute-start(f32[184,640]{1,0:T(8,128)S(1)} %get-tuple-element.23), channel_id=1, source_target_pairs={{0,4},{4,8},{8,12},{12,16},{16,20},{20,24},{24,28},{28,32},{32,36}... | collective-permute-start | bytes 1413128 | tf_op jit(solution)/shard_map/ppermute | solution.py:282
  37.2 10.6 %collective-permute-start.1 = (f32[64,640]{1,0:T(8,128)S(1)}, f32[64,640]{1,0:T(8,128)S(1)}, u32[]{:S(2)}, u32[]{:S(2)}) collective-permute-start(f32[64,640]{1,0:T(8,128)S(1)} %get-tuple-element.24), channel_id=1, source_target_pairs={{4,0},{8,4},{12,8},{16,12},{20,16},{24,20},{28,24},{32,28},{36,32}... | collective-permute-start | bytes 491528 | tf_op jit(solution)/shard_map/ppermute | solution.py:282
  47.7 6.3 %collective-permute-done.1.below = f32[64,640]{1,0:T(8,128)S(1)} collective-permute-done((f32[64,640]{1,0:T(8,128)S(1)}, f32[64,640]{1,0:T(8,128)S(1)}, u32[]{:S(2)}, u32[]{:S(2)}) %collective-permute-start.1) | collective-permute-done | bytes 163872 | tf_op jit(solution)/shard_map/ppermute | solution.py:282
  54.0 4.2 %collective-permute-done.above = f32[184,640]{1,0:T(8,128)S(1)} collective-permute-done((f32[184,640]{1,0:T(8,128)S(1)}, f32[184,640]{1,0:T(8,128)S(1)}, u32[]{:S(2)}, u32[]{:S(2)}) %collective-permute-start) | collective-permute-done | bytes 471072 | tf_op jit(solution)/shard_map/ppermute | solution.py:282
  58.2 6.1 %shard_map.65 = (f32[512,512]{1,0:T(8,128)S(1)}, f32[512,128]{1,0:T(8,128)S(1)}, f32[64,640]{1,0:T(8,128)S(1)}, f32[184,640]{1,0:T(8,128)}) custom-call(s32[8]{0:T(128)S(1)} %copy-done.10, f32[512,512]{1,0:T(8,128)S(1)} %get-tuple-element.21.vectors, f32[512,128]{1,0:T(8,128)S(1)} %get-tuple-element.22.panel, f32[184,640]{1,0:T(8,128)S(1)} %collective-permute-done.above, ...), custom_call_target="tpu_custom_call" | custom-call | tf_op jit(solution)/shard_map/pallas_call | solution.py:235
  65.0 1.9 %collective-permute-start.2 = (f32[184,640]{1,0:T(8,128)}, f32[184,640]{1,0:T(8,128)S(1)}, u32[]{:S(2)}, u32[]{:S(2)}) collective-permute-start(f32[184,640]{1,0:T(8,128)} %get-tuple-element.27), channel_id=1, source_target_pairs={{0,4},{4,8},{8,12},{12,16},{16,20},{20,24},{24,28},{28,32},{32,36}... | collective-permute-start | bytes 1413128 | tf_op jit(solution)/shard_map/ppermute | solution.py:282
  66.9 10.6 %collective-permute-start.3 = (f32[64,640]{1,0:T(8,128)S(1)}, f32[64,640]{1,0:T(8,128)S(1)}, u32[]{:S(2)}, u32[]{:S(2)}) collective-permute-start(f32[64,640]{1,0:T(8,128)S(1)} %get-tuple-element.28), channel_id=1, source_target_pairs={{4,0},{8,4},{12,8},{16,12},{20,16},{24,20},{28,24},{32,28},{36,32}... | collective-permute-start | bytes 491528 | tf_op jit(solution)/shard_map/ppermute | solution.py:282
  77.5 9.5 %collective-permute-done.3.below = f32[64,640]{1,0:T(8,128)S(1)} collective-permute-done((f32[64,640]{1,0:T(8,128)S(1)}, f32[64,640]{1,0:T(8,128)S(1)}, u32[]{:S(2)}, u32[]{:S(2)}) %collective-permute-start.3) | collective-permute-done | bytes 163872 | tf_op jit(solution)/shard_map/ppermute | solution.py:282
  88.5 1.0 copy-done.4
  89.5 0.9 copy-done.7
  90.5 0.9 copy-done.9
  91.4 4.9 %shard_map.66 = (f32[512,512]{1,0:T(8,128)S(1)}, f32[512,512]{1,0:T(8,128)S(1)}, f32[512,128]{1,0:T(8,128)S(1)}, f32[64,512]{1,0:T(8,128)S(1)}, f32[160,512]{1,0:T(8,128)S(1)}) custom-call(s32[8]{0:T(128)S(1)} %copy-done.10, f32[512,512]{1,0:T(8,128)S(1)} %get-tuple-element.25.vectors, f32[512,128]{1,0:T(8,128)S(1)} %copy-done.7, f32[184,640]{1,0:T(8,128)S(1)} %copy-done.4, ...), custom_call_target="tpu_custom_call" | custom-call | tf_op jit(solution)/shard_map/pallas_call | solution.py:235
  97.1 1.4 collective-permute-done.8
  99.2 4.9 %all-to-all-start.1 = ((f32[16,4,640]{2,1,0:T(4,128)}), f32[16,4,640]{2,1,0:T(4,128)S(1)}, u32[]{:S(2)}, u32[]{:S(2)}) async-start(f32[16,4,640]{2,1,0:T(4,128)} %reshape.6), calls=%async_computation.1 | async-start | bytes 327680 | tf_op jit(solution)/shard_map/all_to_all | solution.py:290
  104.1 1.9 %collective-permute-start.4 = (f32[160,512]{1,0:T(8,128)S(1)}, f32[160,512]{1,0:T(8,128)S(1)}, u32[]{:S(2)}, u32[]{:S(2)}) collective-permute-start(f32[160,512]{1,0:T(8,128)S(1)} %copy-done.12), channel_id=1, source_target_pairs={{0,4},{4,8},{8,12},{12,16},{16,20},{20,24},{24,28},{28,32},{32,36}... | collective-permute-start | bytes 983048 | tf_op jit(solution)/shard_map/ppermute | solution.py:282
  106.0 4.5 %all-to-all-done.1 = f32[16,4,640]{2,1,0:T(4,128)S(1)} async-done(((f32[16,4,640]{2,1,0:T(4,128)}), f32[16,4,640]{2,1,0:T(4,128)S(1)}, u32[]{:S(2)}, u32[]{:S(2)}) %all-to-all-start.1) | async-done | bytes 163872 | tf_op jit(solution)/shard_map/all_to_all | solution.py:290
  110.6 9.1 %collective-permute-start.9 = (f32[4,640]{1,0:T(4,128)S(1)}, f32[4,640]{1,0:T(4,128)S(1)}, u32[]{:S(2)}, u32[]{:S(2)}) collective-permute-start(f32[4,640]{1,0:T(4,128)S(1)} %reduce_sum.9), channel_id=1, source_target_pairs={{0,8},{4,12},{8,0},{12,4},{16,24},{20,28},{24,16},{28,20},{32,40},... | collective-permute-start | bytes 30728 | tf_op jit(solution)/shard_map/ppermute | solution.py:286
  119.7 1.9 %collective-permute-done.9 = f32[4,640]{1,0:T(4,128)S(1)} collective-permute-done((f32[4,640]{1,0:T(4,128)S(1)}, f32[4,640]{1,0:T(4,128)S(1)}, u32[]{:S(2)}, u32[]{:S(2)}) %collective-permute-start.9) | collective-permute-done | bytes 10272 | tf_op jit(solution)/shard_map/ppermute | solution.py:286
  121.7 14.0 %all_to_all.16 = f32[16,4,640]{2,1,0:T(4,128)S(1)} all-to-all(f32[16,4,640]{2,1,0:T(4,128)S(1)} %broadcast_in_dim.7), channel_id=1, replica_groups={{0,16,32,48,64,80,96,112,128,144,160,176,192,208,224,240},{4,20,36,52,6..., dimensions={0} | all-to-all | bytes 327680 | tf_op jit(solution)/shard_map/all_to_all | solution.py:290
  135.9 8.3 %collective-permute-start.5 = (f32[64,512]{1,0:T(8,128)S(1)}, f32[64,512]{1,0:T(8,128)S(1)}, u32[]{:S(2)}, u32[]{:S(2)}) collective-permute-start(f32[64,512]{1,0:T(8,128)S(1)} %get-tuple-element.31), channel_id=1, source_target_pairs={{4,0},{8,4},{12,8},{16,12},{20,16},{24,20},{28,24},{32,28},{36,32}... | collective-permute-start | bytes 393224 | tf_op jit(solution)/shard_map/ppermute | solution.py:282
  144.2 2.5 %collective-permute-done.5.below = f32[64,512]{1,0:T(8,128)S(1)} collective-permute-done((f32[64,512]{1,0:T(8,128)S(1)}, f32[64,512]{1,0:T(8,128)S(1)}, u32[]{:S(2)}, u32[]{:S(2)}) %collective-permute-start.5) | collective-permute-done | bytes 131104 | tf_op jit(solution)/shard_map/ppermute | solution.py:282
  146.7 3.6 %shard_map.67 = (f32[512,512]{1,0:T(8,128)S(1)}, f32[64,512]{1,0:T(8,128)S(1)}, f32[160,512]{1,0:T(8,128)S(1)}) custom-call(s32[8]{0:T(128)S(1)} %copy-done.10, f32[512,512]{1,0:T(8,128)S(1)} %get-tuple-element.29.vectors, f32[160,512]{1,0:T(8,128)S(1)} %collective-permute-done.4.above, f32[64,512]{1,0:T(8,128)S(1)} %collective-permute-done.5.below, ...), custom_call_target="tpu_custom_call" | custom-call | tf_op jit(solution)/shard_map/pallas_call | solution.py:235
  150.3 2.7 %collective-permute-start.6 = (f32[160,512]{1,0:T(8,128)S(1)}, f32[160,512]{1,0:T(8,128)S(1)}, u32[]{:S(2)}, u32[]{:S(2)}) collective-permute-start(f32[160,512]{1,0:T(8,128)S(1)} %get-tuple-element.33), channel_id=1, source_target_pairs={{0,4},{4,8},{8,12},{12,16},{16,20},{20,24},{24,28},{28,32},{32,36}... | collective-permute-start | bytes 983048 | tf_op jit(solution)/shard_map/ppermute | solution.py:282
  153.0 9.9 %collective-permute-start.7 = (f32[64,512]{1,0:T(8,128)S(1)}, f32[64,512]{1,0:T(8,128)S(1)}, u32[]{:S(2)}, u32[]{:S(2)}) collective-permute-start(f32[64,512]{1,0:T(8,128)S(1)} %get-tuple-element.34), channel_id=1, source_target_pairs={{4,0},{8,4},{12,8},{16,12},{20,16},{24,20},{28,24},{32,28},{36,32}... | collective-permute-start | bytes 393224 | tf_op jit(solution)/shard_map/ppermute | solution.py:282
  163.0 0.9 broadcast_select_fusion.1
  164.0 2.8 %collective-permute-done.7.below = f32[64,512]{1,0:T(8,128)S(1)} collective-permute-done((f32[64,512]{1,0:T(8,128)S(1)}, f32[64,512]{1,0:T(8,128)S(1)}, u32[]{:S(2)}, u32[]{:S(2)}) %collective-permute-start.7) | collective-permute-done | bytes 131104 | tf_op jit(solution)/shard_map/ppermute | solution.py:282
  166.7 2.9 %collective-permute-done.6.above = f32[160,512]{1,0:T(8,128)S(1)} collective-permute-done((f32[160,512]{1,0:T(8,128)S(1)}, f32[160,512]{1,0:T(8,128)S(1)}, u32[]{:S(2)}, u32[]{:S(2)}) %collective-permute-start.6) | collective-permute-done | bytes 327712 | tf_op jit(solution)/shard_map/ppermute | solution.py:282
  169.6 2.9 %shard_map.68.vectors = f32[512,512]{1,0:T(8,128)S(1)} custom-call(s32[8]{0:T(128)S(1)} %copy-done.10, f32[512,512]{1,0:T(8,128)S(1)} %get-tuple-element.32.vectors, f32[160,512]{1,0:T(8,128)S(1)} %collective-permute-done.6.above, f32[64,512]{1,0:T(8,128)S(1)} %collective-permute-done.7.below, f32[4,2,4,64,128]{4,3,2,1,0:T(8,128)S(1)} %all_to_all.15.p0.p1.q0.q1.p2.p3.q2.q3, ...), custom_call_target="tpu_custom_call" | custom-call | tf_op jit(solution)/shard_map/pallas_call | solution.py:235
  172.5 3.5 %final.1 = f32[512,512]{1,0:T(8,128)} custom-call(f32[512,512]{1,0:T(8,128)S(1)} %shard_map.68.vectors, f32[512,128]{1,0:T(8,128)S(1)} %copy-done.1, f32[128,640]{1,0:T(8,128)S(1)} %pad_maximum_fusion.total), custom_call_target="tpu_custom_call" | custom-call | tf_op jit(solution)/shard_map/final/pallas_call | solution.py:269
  (41 shorter events, 5.8 us)
Async XLA Ops:
  0.0 0.7 copy-start
  0.9 1.2 copy-start.5
  3.0 29.9 %copy-start.1 = (f32[512,128]{1,0:T(8,128)S(1)}, f32[512,128]{1,0:T(8,128)}, u32[]{:S(2)}) copy-start(f32[512,128]{1,0:T(8,128)} %panel.5) | copy-start | bytes 786436
  3.0 29.9 %copy-start.2 = (f32[512,512]{1,0:T(8,128)S(1)}, f32[512,512]{1,0:T(8,128)}, u32[]{:S(2)}) copy-start(f32[512,512]{1,0:T(8,128)} %vectors.1) | copy-start | bytes 3145732
  3.1 29.9 %copy-start.10 = (s32[8]{0:T(128)S(1)}, s32[8]{0:T(128)}, u32[]{:S(2)}) copy-start(s32[8]{0:T(128)} %starts.9) | copy-start | bytes 100
  35.2 23.0 %collective-permute-start = (f32[184,640]{1,0:T(8,128)S(1)}, f32[184,640]{1,0:T(8,128)S(1)}, u32[]{:S(2)}, u32[]{:S(2)}) collective-permute-start(f32[184,640]{1,0:T(8,128)S(1)} %get-tuple-element.23), channel_id=1, source_target_pairs={{0,4},{4,8},{8,12},{12,16},{16,20},{20,24},{24,28},{28,32},{32,36}... | collective-permute-start | bytes 1413128 | tf_op jit(solution)/shard_map/ppermute | solution.py:282
  37.2 16.8 %collective-permute-start.1 = (f32[64,640]{1,0:T(8,128)S(1)}, f32[64,640]{1,0:T(8,128)S(1)}, u32[]{:S(2)}, u32[]{:S(2)}) collective-permute-start(f32[64,640]{1,0:T(8,128)S(1)} %get-tuple-element.24), channel_id=1, source_target_pairs={{4,0},{8,4},{12,8},{16,12},{20,16},{24,20},{28,24},{32,28},{36,32}... | collective-permute-start | bytes 491528 | tf_op jit(solution)/shard_map/ppermute | solution.py:282
  64.3 0.7 copy-start.6
  65.0 22.7 %collective-permute-start.2 = (f32[184,640]{1,0:T(8,128)}, f32[184,640]{1,0:T(8,128)S(1)}, u32[]{:S(2)}, u32[]{:S(2)}) collective-permute-start(f32[184,640]{1,0:T(8,128)} %get-tuple-element.27), channel_id=1, source_target_pairs={{0,4},{4,8},{8,12},{12,16},{16,20},{20,24},{24,28},{28,32},{32,36}... | collective-permute-start | bytes 1413128 | tf_op jit(solution)/shard_map/ppermute | solution.py:282
  66.9 20.1 %collective-permute-start.3 = (f32[64,640]{1,0:T(8,128)S(1)}, f32[64,640]{1,0:T(8,128)S(1)}, u32[]{:S(2)}, u32[]{:S(2)}) collective-permute-start(f32[64,640]{1,0:T(8,128)S(1)} %get-tuple-element.28), channel_id=1, source_target_pairs={{4,0},{8,4},{12,8},{16,12},{20,16},{24,20},{28,24},{32,28},{36,32}... | collective-permute-start | bytes 491528 | tf_op jit(solution)/shard_map/ppermute | solution.py:282
  87.0 0.7 copy-start.8
  87.7 0.8 copy-start.3
  88.5 1.0 copy-start.4
  89.5 0.9 copy-start.7
  90.4 0.9 copy-start.9
  96.3 0.7 copy-start.11
  97.0 1.5 collective-permute-start.8
  98.5 5.6 %copy-start.12 = (f32[160,512]{1,0:T(8,128)S(1)}, f32[160,512]{1,0:T(8,128)}, u32[]{:S(2)}) copy-start(f32[160,512]{1,0:T(8,128)} %copy-done.11) | copy-start | bytes 983044
  99.2 11.3 %all-to-all-start.1 = ((f32[16,4,640]{2,1,0:T(4,128)}), f32[16,4,640]{2,1,0:T(4,128)S(1)}, u32[]{:S(2)}, u32[]{:S(2)}) async-start(f32[16,4,640]{2,1,0:T(4,128)} %reshape.6), calls=%async_computation.1 | async-start | bytes 327680 | tf_op jit(solution)/shard_map/all_to_all | solution.py:290
  104.1 42.6 %collective-permute-start.4 = (f32[160,512]{1,0:T(8,128)S(1)}, f32[160,512]{1,0:T(8,128)S(1)}, u32[]{:S(2)}, u32[]{:S(2)}) collective-permute-start(f32[160,512]{1,0:T(8,128)S(1)} %copy-done.12), channel_id=1, source_target_pairs={{0,4},{4,8},{8,12},{12,16},{16,20},{20,24},{24,28},{28,32},{32,36}... | collective-permute-start | bytes 983048 | tf_op jit(solution)/shard_map/ppermute | solution.py:282
  110.6 11.0 %collective-permute-start.9 = (f32[4,640]{1,0:T(4,128)S(1)}, f32[4,640]{1,0:T(4,128)S(1)}, u32[]{:S(2)}, u32[]{:S(2)}) collective-permute-start(f32[4,640]{1,0:T(4,128)S(1)} %reduce_sum.9), channel_id=1, source_target_pairs={{0,8},{4,12},{8,0},{12,4},{16,24},{20,28},{24,16},{28,20},{32,40},... | collective-permute-start | bytes 30728 | tf_op jit(solution)/shard_map/ppermute | solution.py:286
  135.8 27.2 %collective-permute-start.10 = (f32[64,640]{1,0:T(8,128)S(1)}, f32[64,640]{1,0:T(8,128)}, u32[]{:S(2)}, u32[]{:S(2)}) collective-permute-start(f32[64,640]{1,0:T(8,128)S(1)} %reshape.7), channel_id=1, source_target_pairs={{0,4},{4,0},{8,12},{12,8},{16,20},{20,16},{24,28},{28,24},{32,36},... | collective-permute-start | bytes 491528 | tf_op jit(solution)/shard_map/ppermute | solution.py:286
  135.9 10.8 %collective-permute-start.5 = (f32[64,512]{1,0:T(8,128)S(1)}, f32[64,512]{1,0:T(8,128)S(1)}, u32[]{:S(2)}, u32[]{:S(2)}) collective-permute-start(f32[64,512]{1,0:T(8,128)S(1)} %get-tuple-element.31), channel_id=1, source_target_pairs={{4,0},{8,4},{12,8},{16,12},{20,16},{24,20},{28,24},{32,28},{36,32}... | collective-permute-start | bytes 393224 | tf_op jit(solution)/shard_map/ppermute | solution.py:282
  150.3 19.3 %collective-permute-start.6 = (f32[160,512]{1,0:T(8,128)S(1)}, f32[160,512]{1,0:T(8,128)S(1)}, u32[]{:S(2)}, u32[]{:S(2)}) collective-permute-start(f32[160,512]{1,0:T(8,128)S(1)} %get-tuple-element.33), channel_id=1, source_target_pairs={{0,4},{4,8},{8,12},{12,16},{16,20},{20,24},{24,28},{28,32},{32,36}... | collective-permute-start | bytes 983048 | tf_op jit(solution)/shard_map/ppermute | solution.py:282
  153.0 13.7 %collective-permute-start.7 = (f32[64,512]{1,0:T(8,128)S(1)}, f32[64,512]{1,0:T(8,128)S(1)}, u32[]{:S(2)}, u32[]{:S(2)}) collective-permute-start(f32[64,512]{1,0:T(8,128)S(1)} %get-tuple-element.34), channel_id=1, source_target_pairs={{4,0},{8,4},{12,8},{16,12},{20,16},{24,20},{28,24},{32,28},{36,32}... | collective-permute-start | bytes 393224 | tf_op jit(solution)/shard_map/ppermute | solution.py:282

commit v2 on v0

v2 whole, which is shorter than its diff:
```python
import functools

import jax
import jax.numpy as jnp
from jax import lax
from jax.experimental import pallas as pl
from jax.experimental.pallas import tpu as pltpu
from jax.sharding import PartitionSpec as P

F32 = jnp.float32
BF16 = jnp.bfloat16
BAND = 128
KREF = 64
HALF = 64
ROWS = 512
COLS = 512
ABOVE = BAND
EXT = ABOVE + ROWS + HALF
EXTRA = 2 * KREF * BAND // COLS
DOWN = BAND + EXTRA
VMEM = pl.BlockSpec(memory_space=pltpu.VMEM)
SMEM = pl.BlockSpec(memory_space=pltpu.SMEM)
PARAMS = pltpu.CompilerParams(vmem_limit_bytes=24 * 1024 * 1024)


def halves(value):
    high = value.astype(BF16)
    return high, (value - high.astype(F32)).astype(BF16)


def product(left, right):
    (lh, ll), (rh, rl) = left, right
    dot = functools.partial(jnp.dot, preferred_element_type=F32)
    return dot(lh, rh) + (dot(ll, rh) + dot(lh, rl))


def full_dot(left, right):
    return jnp.dot(left, right, precision=lax.Precision.HIGHEST, preferred_element_type=F32)


def pack_kernel(lens, reflect, factor, out):
    row = lax.broadcasted_iota(jnp.int32, (KREF, BAND), 0)
    lane = lax.broadcasted_iota(jnp.int32, (KREF, BAND), 1)
    below = jnp.zeros((BAND - KREF, KREF), F32)
    for j in range(reflect.shape[0]):
        for b in range(reflect.shape[1]):
            side = jnp.concatenate([factor[j, b], below], axis=0)
            turned = jnp.concatenate([reflect[j, b], side], axis=1).T
            live = jnp.where(lane < lens[j, b], turned[:KREF], 0.0)
            out[j, b] = jnp.where(lane > row, live, turned[KREF:])


def pack(lens, reflect, factor):
    shape = (*reflect.shape[:2], KREF, BAND)
    return pl.pallas_call(
        pack_kernel,
        out_shape=jax.ShapeDtypeStruct(shape, F32),
        in_specs=[SMEM, VMEM, VMEM],
        out_specs=VMEM,
        compiler_params=PARAMS,
        name="pack",
    )(lens, reflect, factor)


def unpacked(tile, start):
    row = lax.broadcasted_iota(jnp.int32, (KREF, BAND), 0)
    lane = lax.broadcasted_iota(jnp.int32, (KREF, BAND), 1)
    vectors = jnp.where(lane > row, tile, jnp.where(lane == row, 1.0, 0.0))
    vectors = pltpu.roll(vectors, start, 1)
    factor = jnp.where(lane <= row, tile, 0.0)[:, :KREF]
    scaled = product(halves(factor), halves(vectors))
    return [[jnp.where(part, v, 0.0) for part in (lane >= start, lane < start)] for v in (vectors, scaled)]


def apply_blocks(tiles, start, packed):
    ready = {j: unpacked(tile, start) for j, tile in packed.items()}
    work = {}
    for j in sorted({*packed, *(j + 1 for j in packed)}):
        parts = [(b, half) for half, b in enumerate((j, j - 1)) if b in packed]
        size = HALF if j not in packed else BAND
        ref, first = tiles[j]
        work[j] = (parts, ref, pl.ds(first, size), size)
    inner = {}
    for parts, ref, place, size in work.values():
        left = jnp.concatenate([ready[b][0][half] for b, half in parts], axis=0)[:, :size]
        got = product(halves(left), halves(ref[place, :]))
        for k, (b, _) in enumerate(parts):
            piece = got[k * KREF : (k + 1) * KREF]
            inner[b] = inner[b] + piece if b in inner else piece
    inner = {b: halves(value) for b, value in inner.items()}
    for parts, ref, place, size in work.values():
        left = jnp.concatenate([ready[b][1][half] for b, half in parts], axis=0).T[:size]
        right = [jnp.concatenate([inner[b][k] for b, _ in parts], axis=0) for k in range(2)]
        ref[place, :] = ref[place, :] - product(halves(left), right)


def tiles_of(own, above=None, below=None):
    tiles = {j + 1: (own, BAND * j) for j in range(ROWS // BAND)}
    tiles[0] = (above, 0)
    tiles[ROWS // BAND + 1] = (below, 0)
    return tiles


def block(packed, sweep, b):
    return packed[sweep // 2, sweep % 2, b]


def send_down(own, message, packed, sweep):
    message[:BAND, :] = own[ROWS - BAND :, :]
    step = KREF * BAND // COLS
    for k in range(2):
        tile = block(packed, sweep + k, 3)
        for q in range(COLS // BAND):
            place = pl.ds(BAND + step * k, step)
            message[place, q * BAND : (q + 1) * BAND] = tile[q * step : (q + 1) * step, :]


def received_tile(message, k):
    step = KREF * BAND // COLS
    rows = pl.ds(BAND + step * k, step)
    parts = [message[rows, q * BAND : (q + 1) * BAND] for q in range(COLS // BAND)]
    return jnp.concatenate(parts, axis=0)


def first_lower(starts, packed, _, own, message):
    apply_blocks(tiles_of(own), starts[0], {3: block(packed, 0, 2)})
    send_down(own, message, packed, 0)


def first_upper(starts, packed, _, own, message):
    apply_blocks(tiles_of(own), starts[0], {j: block(packed, 0, j - 1) for j in (1, 2)})
    message[...] = own[:HALF, :]


def lower(sweep, starts, packed, _, received, own, *rest):
    below = rest[-1]
    below[...] = received[...]
    tiles = tiles_of(own, below=below)
    apply_blocks(tiles, starts[sweep], {4: block(packed, sweep, 3)})
    apply_blocks(tiles, starts[sweep + 1], {j: block(packed, sweep + 1, j - 1) for j in (2, 3, 4)})
    if len(rest) > 1:
        apply_blocks(tiles, starts[sweep + 2], {3: block(packed, sweep + 2, 2)})
        send_down(own, rest[0], packed, sweep + 2)


def upper(sweep, starts, packed, _, received, own, *rest):
    above = rest[-1]
    above[...] = received[:BAND, :]
    tiles = tiles_of(own, above=above)
    apply_blocks(tiles, starts[sweep], {0: received_tile(received, 0)})
    second = {0: received_tile(received, 1), 1: block(packed, sweep + 1, 0)}
    apply_blocks(tiles, starts[sweep + 1], second)
    if len(rest) > 1:
        third = {j: block(packed, sweep + 2, j - 1) for j in (1, 2)}
        apply_blocks(tiles, starts[sweep + 2], third)
        rest[0][...] = own[:HALF, :]


OWN = (ROWS, COLS)
UP = (HALF, COLS)
DOWN = (BAND + 2 * KREF * BAND // COLS, COLS)


def step(kernel, name, message, scratch, starts, packed, vectors, *received):
    out = [OWN] + ([message] if message else [])
    return pl.pallas_call(
        kernel,
        out_shape=[jax.ShapeDtypeStruct(s, F32) for s in out],
        in_specs=[SMEM] + [VMEM] * (2 + len(received)),
        out_specs=[VMEM] * len(out),
        scratch_shapes=[pltpu.VMEM(s, F32) for s in scratch],
        input_output_aliases={2: 0},
        compiler_params=PARAMS,
        name=name,
    )(starts, packed, vectors, *received)


def project_kernel(panel, vectors, partial):
    turned = panel[...].T
    partial[:, :COLS] = product(halves(turned), halves(vectors[...]))
    partial[:, COLS:] = full_dot(turned, panel[...])


def project(panel, vectors):
    return pl.pallas_call(
        project_kernel,
        out_shape=jax.ShapeDtypeStruct((BAND, COLS + BAND), F32),
        in_specs=[VMEM] * 2,
        out_specs=VMEM,
        compiler_params=PARAMS,
        name="project",
    )(panel, vectors)


def final_kernel(vectors, panel, total, out):
    row = lax.broadcasted_iota(jnp.int32, (BAND, BAND), 0)
    lane = lax.broadcasted_iota(jnp.int32, (BAND, BAND), 1)
    gram = total[:, COLS:]
    identity = jnp.where(row == lane, 1.0, 0.0)
    kept = 0.5 * gram * identity
    down = jnp.sum(kept, axis=1, keepdims=True)
    across = jnp.sum(kept, axis=0, keepdims=True)
    powered = jnp.where(lane > row, gram, 0.0) / down
    inverse = identity - powered
    reach = 1
    while reach * 2 < BAND:
        powered = full_dot(powered, powered)
        inverse = full_dot(inverse, identity + powered)
        reach = reach * 2
    inner = product(halves(inverse / across), halves(total[:, :COLS]))
    out[...] = vectors[...] - product(halves(panel[...]), halves(inner))


def final(vectors, panel, total):
    return pl.pallas_call(
        final_kernel,
        out_shape=jax.ShapeDtypeStruct(OWN, F32),
        in_specs=[VMEM] * 3,
        out_specs=VMEM,
        compiler_params=PARAMS,
        name="final",
    )(vectors, panel, total)


def shifted(value, steps):
    count = lax.axis_size("row")
    begin, end = max(0, -steps), min(count, count - steps)
    return lax.ppermute(value, "row", [(k, k + steps) for k in range(begin, end)])


def swapped(value, bit):
    return lax.ppermute(value, "row", [(k, k ^ bit) for k in range(lax.axis_size("row"))])


def spread(value, groups):
    return lax.all_to_all(
        value, "row", split_axis=0, concat_axis=0, tiled=True, axis_index_groups=groups
    )


def row_sum(value):
    count = lax.axis_size("row")
    groups = [list(range(k, count, 4)) for k in range(4)]
    size = count // 4
    core = lax.axis_index("row") % 2
    rows, width = value.shape
    half = rows // 2
    kept = lax.dynamic_slice_in_dim(value, core * half, half, 0)
    given = lax.dynamic_slice_in_dim(value, (1 - core) * half, half, 0)
    kept = kept + swapped(given, 1)
    share = spread(kept.reshape(size, half // size, width), groups).sum(axis=0)
    share = share + swapped(share, 2)
    copies = jnp.broadcast_to(share, (size, *share.shape))
    kept = spread(copies, groups).reshape(half, width)
    other = swapped(kept, 1)
    upper = jnp.where(core == 0, kept, other)
    lower = jnp.where(core == 0, other, kept)
    return jnp.concatenate([upper, lower], axis=0)


def body(sweep_start, block_len, reflectors, tfactors, panel, eigvecs):
    mine = reflectors.shape[0]
    col = lax.axis_index("col")
    lens = lax.dynamic_slice_in_dim(block_len, col * mine, mine, 0)
    packed = pack(lens, reflectors, tfactors)
    copies = jnp.broadcast_to(packed, (lax.axis_size("col"), *packed.shape))
    packed = lax.all_to_all(copies, "col", split_axis=0, concat_axis=0, tiled=True)
    sweeps = mine * lax.axis_size("col")
    fixed = (sweep_start, packed)
    vectors, downward = step(first_lower, "first_lower", DOWN, (), *fixed, eigvecs)
    from_above = shifted(downward, 1)
    vectors, upward = step(first_upper, "first_upper", UP, (), *fixed, vectors)
    from_below = shifted(upward, -1)
    for sweep in range(0, sweeps - 2, 2):
        kernel = functools.partial(lower, sweep)
        vectors, downward = step(kernel, "lower", DOWN, (UP,), *fixed, vectors, from_below)
        later = shifted(downward, 1)
        kernel = functools.partial(upper, sweep)
        above = (BAND, COLS)
        vectors, upward = step(kernel, "upper", UP, (above,), *fixed, vectors, from_above)
        from_below = shifted(upward, -1)
        from_above = later
    kernel = functools.partial(lower, sweeps - 2)
    (vectors,) = step(kernel, "last_lower", None, (UP,), *fixed, vectors, from_below)
    kernel = functools.partial(upper, sweeps - 2)
    (vectors,) = step(kernel, "last_upper", None, ((BAND, COLS),), *fixed, vectors, from_above)
    return final(vectors, panel, row_sum(project(panel, vectors)))


def solution(mesh):
    in_specs = (
        P(),
        P(None, "row"),
        P("col", "row", None, None),
        P("col", "row", None, None),
        P("row", None),
        P("row", "col"),
    )
    out_specs = P("row", "col")
    return jax.shard_map(body, mesh=mesh, in_specs=in_specs, out_specs=out_specs, check_vma=False)
```

time: 170 us -> 162 us (0.953)
  Pallas kernels: 21.1 us -> 27.2 us
  waiting for transfers between devices: 47.1 us -> 41.8 us
  starting transfers between devices: 37.3 us -> 32.6 us
  local copies, waits for them, and re-layouts: 4.73 us -> 2.67 us
    pallas_call x5 -> x11, Pallas kernels: 16.8 us -> 22.9 us  [the longest x10 22.2 us: step(): pl.pallas_call(kernel, out_shape=[jax.ShapeDtypeStruct(s, F32) for s in o...]
    ppermute x8, waiting for transfers between devices: 43.6 us -> 38.3 us  [shifted(): lax.ppermute(value, 'row', [(k, k + steps) for k in range(begin, end)])]
    ppermute x8, starting transfers between devices: 26.2 us -> 22.9 us  [shifted(): lax.ppermute(value, 'row', [(k, k + steps) for k in range(begin, end)])]
    unnamed x18 -> x13, local copies, waits for them, and re-layouts: 4.41 us -> 2.33 us
  transfers between devices with their start and end apart: 11 -> 11, of which waited for: 7 -> 7; matrix products, arithmetic and copies ran while one was open for 0% -> 0% of each run, Pallas kernels for 0% -> 12%
where the time goes in v2:
time: 162 us; the launch traced here: 161 us
  blocking collectives  56.6 us (35%)
  waiting for transfers between devices  41.8 us (26%)
  starting transfers between devices  32.6 us (20%)
  Pallas kernels  27.2 us (17%)
  local copies, waits for them, and re-layouts  2.67 us (2%)
    ppermute x8, waiting for transfers between devices, shifted(): lax.ppermute(value, 'row', [(k, k + steps) for k in range(begin, end)])  38.3 us
    all_to_all x1, blocking collectives, body(): lax.all_to_all(copies, 'col', split_axis=0, concat_axis=0, tiled=True)  31.2 us
    all_to_all x2, blocking collectives, spread(): lax.all_to_all(value, 'row', split_axis=0, concat_axis=0, tiled=True, axi...  25.4 us
    ppermute x8, starting transfers between devices, shifted(): lax.ppermute(value, 'row', [(k, k + steps) for k in range(begin, end)])  22.9 us
    pallas_call x10, Pallas kernels, step(): pl.pallas_call(kernel, out_shape=[jax.ShapeDtypeStruct(s, F32) for s in o...  22.2 us
    ppermute x3, starting transfers between devices, swapped(): lax.ppermute(value, 'row', [(k, k ^ bit) for k in range(lax.axis_size('ro...  9.67 us
    pallas_call x1, Pallas kernels, final(): pl.pallas_call(final_kernel, out_shape=jax.ShapeDtypeStruct(OWN, F32), in...  3.49 us
    ppermute x3, waiting for transfers between devices, swapped(): lax.ppermute(value, 'row', [(k, k ^ bit) for k in range(lax.axis_size('ro...  3.47 us
  transfers between devices with their start and end apart: 11, of which 7 were waited for; matrix products, arithmetic and copies ran while one was open for 0% of the time, Pallas kernels for 12%

profile of v2, /device:TPU:1, one launch (start us, length us, event | category | flops | bytes accessed | tf_op | source)
XLA Modules:
  0.0 161.2 jit_solution(12624038171272465597)
XLA Ops:
  0.0 1.3 copy.31._
  3.4 31.2 %all_to_all.17.packed = f32[4,2,4,64,128]{4,3,2,1,0:T(8,128)S(1)} all-to-all(f32[4,2,4,64,128]{4,3,2,1,0:T(8,128)S(1)} %broadcast_in_dim.6), channel_id=1, replica_groups=mesh['row'=64,'col'=4] {'col'}, dimensions={0} | all-to-all | bytes 2097152 | tf_op jit(solution)/shard_map/all_to_all | solution.py:267
  34.5 1.3 first_lower.1
  35.9 7.8 %collective-permute-start.1 = (f32[160,512]{1,0:T(8,128)S(1)}, f32[160,512]{1,0:T(8,128)S(1)}, u32[]{:S(2)}, u32[]{:S(2)}) collective-permute-start(f32[160,512]{1,0:T(8,128)S(1)} %get-tuple-element.25), channel_id=1, source_target_pairs={{0,4},{4,8},{8,12},{12,16},{16,20},{20,24},{24,28},{28,32},{32,36}... | collective-permute-start | bytes 983048 | tf_op jit(solution)/shard_map/ppermute | solution.py:228
  43.7 1.4 first_upper.1
  45.0 1.9 %collective-permute-start = (f32[64,512]{1,0:T(8,128)S(1)}, f32[64,512]{1,0:T(8,128)S(1)}, u32[]{:S(2)}, u32[]{:S(2)}) collective-permute-start(f32[64,512]{1,0:T(8,128)S(1)} %get-tuple-element.23), channel_id=1, source_target_pairs={{4,0},{8,4},{12,8},{16,12},{20,16},{24,20},{28,24},{32,28},{36,32}... | collective-permute-start | bytes 393224 | tf_op jit(solution)/shard_map/ppermute | solution.py:228
  47.0 8.3 %collective-permute-done.received = f32[64,512]{1,0:T(8,128)S(1)} collective-permute-done((f32[64,512]{1,0:T(8,128)S(1)}, f32[64,512]{1,0:T(8,128)S(1)}, u32[]{:S(2)}, u32[]{:S(2)}) %collective-permute-start) | collective-permute-done | bytes 131104 | tf_op jit(solution)/shard_map/ppermute | solution.py:228
  55.3 2.6 %lower.3 = (f32[512,512]{1,0:T(8,128)S(1)}, f32[160,512]{1,0:T(8,128)S(1)}) custom-call(s32[8]{0:T(128)S(1)} %copy-done.3, f32[4,2,4,64,128]{4,3,2,1,0:T(8,128)S(1)} %all_to_all.17.packed, f32[512,512]{1,0:T(8,128)S(1)} %get-tuple-element.22._, f32[64,512]{1,0:T(8,128)S(1)} %collective-permute-done.received), custom_call_target="tpu_custom_call", output_to_operand_aliasing={{0}: (2, {})} | custom-call | tf_op jit(solution)/shard_map/lower/pallas_call | solution.py:166
  57.9 1.9 %collective-permute-start.3 = (f32[160,512]{1,0:T(8,128)S(1)}, f32[160,512]{1,0:T(8,128)S(1)}, u32[]{:S(2)}, u32[]{:S(2)}) collective-permute-start(f32[160,512]{1,0:T(8,128)S(1)} %get-tuple-element.29), channel_id=1, source_target_pairs={{0,4},{4,8},{8,12},{12,16},{16,20},{20,24},{24,28},{28,32},{32,36}... | collective-permute-start | bytes 983048 | tf_op jit(solution)/shard_map/ppermute | solution.py:228
  59.8 2.6 %upper.3 = (f32[512,512]{1,0:T(8,128)S(1)}, f32[64,512]{1,0:T(8,128)S(1)}) custom-call(s32[8]{0:T(128)S(1)} %copy-done.3, f32[4,2,4,64,128]{4,3,2,1,0:T(8,128)S(1)} %all_to_all.17.packed, f32[512,512]{1,0:T(8,128)S(1)} %get-tuple-element.24._, f32[160,512]{1,0:T(8,128)S(1)} %collective-permute-done.1.received), custom_call_target="tpu_custom_call", output_to_operand_aliasing={{0}: (2, {})} | custom-call | tf_op jit(solution)/shard_map/upper/pallas_call | solution.py:166
  62.4 2.4 %collective-permute-start.2 = (f32[64,512]{1,0:T(8,128)S(1)}, f32[64,512]{1,0:T(8,128)S(1)}, u32[]{:S(2)}, u32[]{:S(2)}) collective-permute-start(f32[64,512]{1,0:T(8,128)S(1)} %get-tuple-element.27), channel_id=1, source_target_pairs={{4,0},{8,4},{12,8},{16,12},{20,16},{24,20},{28,24},{32,28},{36,32}... | collective-permute-start | bytes 393224 | tf_op jit(solution)/shard_map/ppermute | solution.py:228
  64.8 9.5 %collective-permute-done.2.received = f32[64,512]{1,0:T(8,128)S(1)} collective-permute-done((f32[64,512]{1,0:T(8,128)S(1)}, f32[64,512]{1,0:T(8,128)S(1)}, u32[]{:S(2)}, u32[]{:S(2)}) %collective-permute-start.2) | collective-permute-done | bytes 131104 | tf_op jit(solution)/shard_map/ppermute | solution.py:228
  74.4 2.6 %lower.4 = (f32[512,512]{1,0:T(8,128)S(1)}, f32[160,512]{1,0:T(8,128)S(1)}) custom-call(s32[8]{0:T(128)S(1)} %copy-done.3, f32[4,2,4,64,128]{4,3,2,1,0:T(8,128)S(1)} %all_to_all.17.packed, f32[512,512]{1,0:T(8,128)S(1)} %get-tuple-element.26._, f32[64,512]{1,0:T(8,128)S(1)} %collective-permute-done.2.received), custom_call_target="tpu_custom_call", output_to_operand_aliasing={{0}: (2, {})} | custom-call | tf_op jit(solution)/shard_map/lower/pallas_call | solution.py:166
  77.0 1.9 %collective-permute-start.5 = (f32[160,512]{1,0:T(8,128)S(1)}, f32[160,512]{1,0:T(8,128)S(1)}, u32[]{:S(2)}, u32[]{:S(2)}) collective-permute-start(f32[160,512]{1,0:T(8,128)S(1)} %get-tuple-element.33), channel_id=1, source_target_pairs={{0,4},{4,8},{8,12},{12,16},{16,20},{20,24},{24,28},{28,32},{32,36}... | collective-permute-start | bytes 983048 | tf_op jit(solution)/shard_map/ppermute | solution.py:228
  78.9 2.6 %upper.4 = (f32[512,512]{1,0:T(8,128)S(1)}, f32[64,512]{1,0:T(8,128)S(1)}) custom-call(s32[8]{0:T(128)S(1)} %copy-done.3, f32[4,2,4,64,128]{4,3,2,1,0:T(8,128)S(1)} %all_to_all.17.packed, f32[512,512]{1,0:T(8,128)S(1)} %get-tuple-element.28._, f32[160,512]{1,0:T(8,128)S(1)} %collective-permute-done.3.received), custom_call_target="tpu_custom_call", output_to_operand_aliasing={{0}: (2, {})} | custom-call | tf_op jit(solution)/shard_map/upper/pallas_call | solution.py:166
  81.5 2.4 %collective-permute-start.4 = (f32[64,512]{1,0:T(8,128)S(1)}, f32[64,512]{1,0:T(8,128)S(1)}, u32[]{:S(2)}, u32[]{:S(2)}) collective-permute-start(f32[64,512]{1,0:T(8,128)S(1)} %get-tuple-element.31), channel_id=1, source_target_pairs={{4,0},{8,4},{12,8},{16,12},{20,16},{24,20},{28,24},{32,28},{36,32}... | collective-permute-start | bytes 393224 | tf_op jit(solution)/shard_map/ppermute | solution.py:228
  83.9 10.2 %collective-permute-done.4.received = f32[64,512]{1,0:T(8,128)S(1)} collective-permute-done((f32[64,512]{1,0:T(8,128)S(1)}, f32[64,512]{1,0:T(8,128)S(1)}, u32[]{:S(2)}, u32[]{:S(2)}) %collective-permute-start.4) | collective-permute-done | bytes 131104 | tf_op jit(solution)/shard_map/ppermute | solution.py:228
  94.1 2.6 %lower.5 = (f32[512,512]{1,0:T(8,128)S(1)}, f32[160,512]{1,0:T(8,128)S(1)}) custom-call(s32[8]{0:T(128)S(1)} %copy-done.3, f32[4,2,4,64,128]{4,3,2,1,0:T(8,128)S(1)} %all_to_all.17.packed, f32[512,512]{1,0:T(8,128)S(1)} %get-tuple-element.30._, f32[64,512]{1,0:T(8,128)S(1)} %collective-permute-done.4.received), custom_call_target="tpu_custom_call", output_to_operand_aliasing={{0}: (2, {})} | custom-call | tf_op jit(solution)/shard_map/lower/pallas_call | solution.py:166
  96.8 1.9 %collective-permute-start.7 = (f32[160,512]{1,0:T(8,128)S(1)}, f32[160,512]{1,0:T(8,128)S(1)}, u32[]{:S(2)}, u32[]{:S(2)}) collective-permute-start(f32[160,512]{1,0:T(8,128)S(1)} %get-tuple-element.36), channel_id=1, source_target_pairs={{0,4},{4,8},{8,12},{12,16},{16,20},{20,24},{24,28},{28,32},{32,36}... | collective-permute-start | bytes 983048 | tf_op jit(solution)/shard_map/ppermute | solution.py:228
  98.7 2.6 %upper.5 = (f32[512,512]{1,0:T(8,128)S(1)}, f32[64,512]{1,0:T(8,128)S(1)}) custom-call(s32[8]{0:T(128)S(1)} %copy-done.3, f32[4,2,4,64,128]{4,3,2,1,0:T(8,128)S(1)} %all_to_all.17.packed, f32[512,512]{1,0:T(8,128)S(1)} %get-tuple-element.32._, f32[160,512]{1,0:T(8,128)S(1)} %collective-permute-done.5.received), custom_call_target="tpu_custom_call", output_to_operand_aliasing={{0}: (2, {})} | custom-call | tf_op jit(solution)/shard_map/upper/pallas_call | solution.py:166
  101.3 2.6 %collective-permute-start.6 = (f32[64,512]{1,0:T(8,128)S(1)}, f32[64,512]{1,0:T(8,128)S(1)}, u32[]{:S(2)}, u32[]{:S(2)}) collective-permute-start(f32[64,512]{1,0:T(8,128)S(1)} %get-tuple-element.35), channel_id=1, source_target_pairs={{4,0},{8,4},{12,8},{16,12},{20,16},{24,20},{28,24},{32,28},{36,32}... | collective-permute-start | bytes 393224 | tf_op jit(solution)/shard_map/ppermute | solution.py:228
  103.9 10.2 %collective-permute-done.6.received = f32[64,512]{1,0:T(8,128)S(1)} collective-permute-done((f32[64,512]{1,0:T(8,128)S(1)}, f32[64,512]{1,0:T(8,128)S(1)}, u32[]{:S(2)}, u32[]{:S(2)}) %collective-permute-start.6) | collective-permute-done | bytes 131104 | tf_op jit(solution)/shard_map/ppermute | solution.py:228
  114.1 2.0 %last_lower.1._ = f32[512,512]{1,0:T(8,128)S(1)} custom-call(s32[8]{0:T(128)S(1)} %copy-done.3, f32[4,2,4,64,128]{4,3,2,1,0:T(8,128)S(1)} %all_to_all.17.packed, f32[512,512]{1,0:T(8,128)S(1)} %get-tuple-element.34._, f32[64,512]{1,0:T(8,128)S(1)} %collective-permute-done.6.received), custom_call_target="tpu_custom_call", output_to_operand_aliasing={{}: (2, {})} | custom-call | tf_op jit(solution)/shard_map/last_lower/pallas_call | solution.py:166
  116.2 2.0 %last_upper.1.vectors = f32[512,512]{1,0:T(8,128)S(1)} custom-call(s32[8]{0:T(128)S(1)} %copy-done.3, f32[4,2,4,64,128]{4,3,2,1,0:T(8,128)S(1)} %all_to_all.17.packed, f32[512,512]{1,0:T(8,128)S(1)} %last_lower.1._, f32[160,512]{1,0:T(8,128)S(1)} %collective-permute-done.7.received), custom_call_target="tpu_custom_call", output_to_operand_aliasing={{}: (2, {})} | custom-call | tf_op jit(solution)/shard_map/last_upper/pallas_call | solution.py:166
  119.0 1.4 collective-permute-done.8
  120.4 15.2 %all_to_all.15 = f32[16,4,640]{2,1,0:T(4,128)S(1)} all-to-all(f32[16,4,640]{2,1,0:T(4,128)S(1)} %reshape.6), channel_id=1, replica_groups={{0,16,32,48,64,80,96,112,128,144,160,176,192,208,224,240},{4,20,36,52,6..., dimensions={0} | all-to-all | bytes 327680 | tf_op jit(solution)/shard_map/all_to_all | solution.py:236
  135.7 5.9 %collective-permute-start.9 = (f32[4,640]{1,0:T(4,128)S(1)}, f32[4,640]{1,0:T(4,128)S(1)}, u32[]{:S(2)}, u32[]{:S(2)}) collective-permute-start(f32[4,640]{1,0:T(4,128)S(1)} %reduce_sum.9), channel_id=1, source_target_pairs={{0,8},{4,12},{8,0},{12,4},{16,24},{20,28},{24,16},{28,20},{32,40},... | collective-permute-start | bytes 30728 | tf_op jit(solution)/shard_map/ppermute | solution.py:232
  141.5 1.1 collective-permute-done.9
  142.6 10.2 %all_to_all.16 = f32[16,4,640]{2,1,0:T(4,128)S(1)} all-to-all(f32[16,4,640]{2,1,0:T(4,128)S(1)} %broadcast_in_dim.7), channel_id=1, replica_groups={{0,16,32,48,64,80,96,112,128,144,160,176,192,208,224,240},{4,20,36,52,6..., dimensions={0} | all-to-all | bytes 327680 | tf_op jit(solution)/shard_map/all_to_all | solution.py:236
  152.9 3.7 %collective-permute-start.10 = (f32[64,640]{1,0:T(8,128)S(1)}, f32[64,640]{1,0:T(8,128)S(1)}, u32[]{:S(2)}, u32[]{:S(2)}) collective-permute-start(f32[64,640]{1,0:T(8,128)S(1)} %reshape.7), channel_id=1, source_target_pairs={{0,4},{4,0},{8,12},{12,8},{16,20},{20,16},{24,28},{28,24},{32,36},... | collective-permute-start | bytes 491528 | tf_op jit(solution)/shard_map/ppermute | solution.py:232
  156.6 1.0 collective-permute-done.10
  157.7 3.5 %final.1 = f32[512,512]{1,0:T(8,128)} custom-call(f32[512,512]{1,0:T(8,128)S(1)} %last_upper.1.vectors, f32[512,128]{1,0:T(8,128)S(1)} %copy-done.1, f32[128,640]{1,0:T(8,128)S(1)} %pad_maximum_fusion.total), custom_call_target="tpu_custom_call" | custom-call | tf_op jit(solution)/shard_map/final/pallas_call | solution.py:215
  (30 shorter events, 3.1 us)
Async XLA Ops:
  0.0 1.3 copy-start
  0.0 1.4 copy-start.4
  1.4 1.0 copy-start.2
  3.4 31.2 %copy-start.3 = (s32[8]{0:T(128)S(1)}, s32[8]{0:T(128)}, u32[]{:S(2)}) copy-start(s32[8]{0:T(128)} %starts.19) | copy-start | bytes 100
  35.9 23.9 %collective-permute-start.1 = (f32[160,512]{1,0:T(8,128)S(1)}, f32[160,512]{1,0:T(8,128)S(1)}, u32[]{:S(2)}, u32[]{:S(2)}) collective-permute-start(f32[160,512]{1,0:T(8,128)S(1)} %get-tuple-element.25), channel_id=1, source_target_pairs={{0,4},{4,8},{8,12},{12,16},{16,20},{20,24},{24,28},{28,32},{32,36}... | collective-permute-start | bytes 983048 | tf_op jit(solution)/shard_map/ppermute | solution.py:228
  45.0 10.3 %collective-permute-start = (f32[64,512]{1,0:T(8,128)S(1)}, f32[64,512]{1,0:T(8,128)S(1)}, u32[]{:S(2)}, u32[]{:S(2)}) collective-permute-start(f32[64,512]{1,0:T(8,128)S(1)} %get-tuple-element.23), channel_id=1, source_target_pairs={{4,0},{8,4},{12,8},{16,12},{20,16},{24,20},{28,24},{32,28},{36,32}... | collective-permute-start | bytes 393224 | tf_op jit(solution)/shard_map/ppermute | solution.py:228
  57.9 21.0 %collective-permute-start.3 = (f32[160,512]{1,0:T(8,128)S(1)}, f32[160,512]{1,0:T(8,128)S(1)}, u32[]{:S(2)}, u32[]{:S(2)}) collective-permute-start(f32[160,512]{1,0:T(8,128)S(1)} %get-tuple-element.29), channel_id=1, source_target_pairs={{0,4},{4,8},{8,12},{12,16},{16,20},{20,24},{24,28},{28,32},{32,36}... | collective-permute-start | bytes 983048 | tf_op jit(solution)/shard_map/ppermute | solution.py:228
  62.4 12.0 %collective-permute-start.2 = (f32[64,512]{1,0:T(8,128)S(1)}, f32[64,512]{1,0:T(8,128)S(1)}, u32[]{:S(2)}, u32[]{:S(2)}) collective-permute-start(f32[64,512]{1,0:T(8,128)S(1)} %get-tuple-element.27), channel_id=1, source_target_pairs={{4,0},{8,4},{12,8},{16,12},{20,16},{24,20},{28,24},{32,28},{36,32}... | collective-permute-start | bytes 393224 | tf_op jit(solution)/shard_map/ppermute | solution.py:228
  77.0 21.7 %collective-permute-start.5 = (f32[160,512]{1,0:T(8,128)S(1)}, f32[160,512]{1,0:T(8,128)S(1)}, u32[]{:S(2)}, u32[]{:S(2)}) collective-permute-start(f32[160,512]{1,0:T(8,128)S(1)} %get-tuple-element.33), channel_id=1, source_target_pairs={{0,4},{4,8},{8,12},{12,16},{16,20},{20,24},{24,28},{28,32},{32,36}... | collective-permute-start | bytes 983048 | tf_op jit(solution)/shard_map/ppermute | solution.py:228
  81.5 12.6 %collective-permute-start.4 = (f32[64,512]{1,0:T(8,128)S(1)}, f32[64,512]{1,0:T(8,128)S(1)}, u32[]{:S(2)}, u32[]{:S(2)}) collective-permute-start(f32[64,512]{1,0:T(8,128)S(1)} %get-tuple-element.31), channel_id=1, source_target_pairs={{4,0},{8,4},{12,8},{16,12},{20,16},{24,20},{28,24},{32,28},{36,32}... | collective-permute-start | bytes 393224 | tf_op jit(solution)/shard_map/ppermute | solution.py:228
  96.8 19.4 %collective-permute-start.7 = (f32[160,512]{1,0:T(8,128)S(1)}, f32[160,512]{1,0:T(8,128)S(1)}, u32[]{:S(2)}, u32[]{:S(2)}) collective-permute-start(f32[160,512]{1,0:T(8,128)S(1)} %get-tuple-element.36), channel_id=1, source_target_pairs={{0,4},{4,8},{8,12},{12,16},{16,20},{20,24},{24,28},{28,32},{32,36}... | collective-permute-start | bytes 983048 | tf_op jit(solution)/shard_map/ppermute | solution.py:228
  101.3 12.9 %collective-permute-start.6 = (f32[64,512]{1,0:T(8,128)S(1)}, f32[64,512]{1,0:T(8,128)S(1)}, u32[]{:S(2)}, u32[]{:S(2)}) collective-permute-start(f32[64,512]{1,0:T(8,128)S(1)} %get-tuple-element.35), channel_id=1, source_target_pairs={{4,0},{8,4},{12,8},{16,12},{20,16},{24,20},{28,24},{32,28},{36,32}... | collective-permute-start | bytes 393224 | tf_op jit(solution)/shard_map/ppermute | solution.py:228
  116.2 2.0 %copy-start.1 = (f32[512,128]{1,0:T(8,128)S(1)}, f32[512,128]{1,0:T(8,128)}, u32[]{:S(2)}) copy-start(f32[512,128]{1,0:T(8,128)} %panel.3) | copy-start | bytes 786436
  118.9 1.5 collective-permute-start.8
  135.7 6.9 %collective-permute-start.9 = (f32[4,640]{1,0:T(4,128)S(1)}, f32[4,640]{1,0:T(4,128)S(1)}, u32[]{:S(2)}, u32[]{:S(2)}) collective-permute-start(f32[4,640]{1,0:T(4,128)S(1)} %reduce_sum.9), channel_id=1, source_target_pairs={{0,8},{4,12},{8,0},{12,4},{16,24},{20,28},{24,16},{28,20},{32,40},... | collective-permute-start | bytes 30728 | tf_op jit(solution)/shard_map/ppermute | solution.py:232
  152.9 4.7 %collective-permute-start.10 = (f32[64,640]{1,0:T(8,128)S(1)}, f32[64,640]{1,0:T(8,128)S(1)}, u32[]{:S(2)}, u32[]{:S(2)}) collective-permute-start(f32[64,640]{1,0:T(8,128)S(1)} %reshape.7), channel_id=1, source_target_pairs={{0,4},{4,0},{8,12},{12,8},{16,20},{20,16},{24,28},{28,24},{32,36},... | collective-permute-start | bytes 491528 | tf_op jit(solution)/shard_map/ppermute | solution.py:232

commit v3 on v2

--- a/solution.py
+++ b/solution.py
@@ -14,10 +14,6 @@
 HALF = 64
 ROWS = 512
 COLS = 512
-ABOVE = BAND
-EXT = ABOVE + ROWS + HALF
-EXTRA = 2 * KREF * BAND // COLS
-DOWN = BAND + EXTRA
 VMEM = pl.BlockSpec(memory_space=pltpu.VMEM)
 SMEM = pl.BlockSpec(memory_space=pltpu.SMEM)
 PARAMS = pltpu.CompilerParams(vmem_limit_bytes=24 * 1024 * 1024)
@@ -31,7 +27,7 @@
 def product(left, right):
     (lh, ll), (rh, rl) = left, right
     dot = functools.partial(jnp.dot, preferred_element_type=F32)
-    return dot(lh, rh) + (dot(ll, rh) + dot(lh, rl))
+    return dot(jnp.concatenate([lh, ll, lh], axis=1), jnp.concatenate([rh, rh, rl], axis=0))
 
 
 def full_dot(left, right):
@@ -72,26 +68,74 @@
     return [[jnp.where(part, v, 0.0) for part in (lane >= start, lane < start)] for v in (vectors, scaled)]
 
 
-def apply_blocks(tiles, start, packed):
-    ready = {j: unpacked(tile, start) for j, tile in packed.items()}
-    work = {}
-    for j in sorted({*packed, *(j + 1 for j in packed)}):
-        parts = [(b, half) for half, b in enumerate((j, j - 1)) if b in packed]
-        size = HALF if j not in packed else BAND
-        ref, first = tiles[j]
-        work[j] = (parts, ref, pl.ds(first, size), size)
-    inner = {}
-    for parts, ref, place, size in work.values():
-        left = jnp.concatenate([ready[b][0][half] for b, half in parts], axis=0)[:, :size]
-        got = product(halves(left), halves(ref[place, :]))
-        for k, (b, _) in enumerate(parts):
-            piece = got[k * KREF : (k + 1) * KREF]
-            inner[b] = inner[b] + piece if b in inner else piece
-    inner = {b: halves(value) for b, value in inner.items()}
-    for parts, ref, place, size in work.values():
-        left = jnp.concatenate([ready[b][1][half] for b, half in parts], axis=0).T[:size]
-        right = [jnp.concatenate([inner[b][k] for b, _ in parts], axis=0) for k in range(2)]
-        ref[place, :] = ref[place, :] - product(halves(left), right)
+def plan(blocks):
+    work = []
+    for j in sorted({*blocks, *(j + 1 for j in blocks)}):
+        parts = [(b, half) for half, b in enumerate((j, j - 1)) if b in blocks]
+        work.append((j, parts, BAND if j in blocks else HALF))
+    return work
+
+
+def tripled(left):
+    high, low = halves(left)
+    return jnp.concatenate([high, low, high], axis=1)
+
+
+def prepare_kernel(groups, starts, packed, *rest):
+    front, back = rest[-2:]
+    n = 0
+    for sweep, blocks in groups:
+        ready = {}
+        for j, b in blocks.items():
+            tile = packed[sweep // 2, sweep % 2, b] if j > 0 else received_tile(rest[0], b)
+            ready[j] = unpacked(tile, starts[sweep])
+        for _, parts, size in plan(blocks):
+            span = KREF * len(parts)
+            left = jnp.concatenate([ready[b][0][half] for b, half in parts], axis=0)
+            front[n, :span, : 3 * size] = tripled(left[:, :size])
+            left = jnp.concatenate([ready[b][1][half] for b, half in parts], axis=0).T
+            back[n, :size, : 3 * span] = tripled(left[:size])
+            n += 1
+
+
+def prepare(groups, *operands):
+    count = sum(len(plan(blocks)) for _, blocks in groups)
+    shape = jax.ShapeDtypeStruct((count, BAND, 3 * BAND), BF16)
+    return pl.pallas_call(
+        functools.partial(prepare_kernel, groups),
+        out_shape=[shape] * 2,
+        in_specs=[SMEM] + [VMEM] * (len(operands) - 1),
+        out_specs=[VMEM] * 2,
+        compiler_params=PARAMS,
+        name="prepare",
+    )(*operands)
+
+
+def stacked(value):
+    high, low = halves(value)
+    return jnp.concatenate([high, high, low], axis=0)
+
+
+def apply_groups(tiles, groups, front, back):
+    n = 0
+    for _, blocks in groups:
+        work = plan(blocks)
+        inner = {}
+        for k, (j, parts, size) in enumerate(work):
+            ref, first = tiles[j]
+            left = front[n + k, : KREF * len(parts), : 3 * size]
+            right = stacked(ref[pl.ds(first, size), :])
+            got = jnp.dot(left, right, preferred_element_type=F32)
+            for m, (b, _) in enumerate(parts):
+                piece = got[m * KREF : (m + 1) * KREF]
+                inner[b] = inner[b] + piece if b in inner else piece
+        for k, (j, parts, size) in enumerate(work):
+            ref, first = tiles[j]
+            left = back[n + k, :size, : 3 * KREF * len(parts)]
+            right = stacked(jnp.concatenate([inner[b] for b, _ in parts], axis=0))
+            place = pl.ds(first, size)
+            ref[place, :] = ref[place, :] - jnp.dot(left, right, preferred_element_type=F32)
+        n += len(work)
 
 
 def tiles_of(own, above=None, below=None):
@@ -101,15 +145,15 @@
     return tiles
 
 
-def block(packed, sweep, b):
-    return packed[sweep // 2, sweep % 2, b]
-
-
-def send_down(own, message, packed, sweep):
+def down_rows(count):
+    return BAND + count * KREF * BAND // COLS
+
+
+def send_down(own, message, packed, sweeps):
     message[:BAND, :] = own[ROWS - BAND :, :]
     step = KREF * BAND // COLS
-    for k in range(2):
-        tile = block(packed, sweep + k, 3)
+    for k, sweep in enumerate(sweeps):
+        tile = packed[sweep // 2, sweep % 2, 3]
         for q in range(COLS // BAND):
             place = pl.ds(BAND + step * k, step)
             message[place, q * BAND : (q + 1) * BAND] = tile[q * step : (q + 1) * step, :]
@@ -122,57 +166,49 @@
     return jnp.concatenate(parts, axis=0)
 
 
-def first_lower(starts, packed, _, own, message):
-    apply_blocks(tiles_of(own), starts[0], {3: block(packed, 0, 2)})
-    send_down(own, message, packed, 0)
-
-
-def first_upper(starts, packed, _, own, message):
-    apply_blocks(tiles_of(own), starts[0], {j: block(packed, 0, j - 1) for j in (1, 2)})
-    message[...] = own[:HALF, :]
-
-
-def lower(sweep, starts, packed, _, received, own, *rest):
-    below = rest[-1]
-    below[...] = received[...]
-    tiles = tiles_of(own, below=below)
-    apply_blocks(tiles, starts[sweep], {4: block(packed, sweep, 3)})
-    apply_blocks(tiles, starts[sweep + 1], {j: block(packed, sweep + 1, j - 1) for j in (2, 3, 4)})
-    if len(rest) > 1:
-        apply_blocks(tiles, starts[sweep + 2], {3: block(packed, sweep + 2, 2)})
-        send_down(own, rest[0], packed, sweep + 2)
-
-
-def upper(sweep, starts, packed, _, received, own, *rest):
-    above = rest[-1]
-    above[...] = received[:BAND, :]
-    tiles = tiles_of(own, above=above)
-    apply_blocks(tiles, starts[sweep], {0: received_tile(received, 0)})
-    second = {0: received_tile(received, 1), 1: block(packed, sweep + 1, 0)}
-    apply_blocks(tiles, starts[sweep + 1], second)
-    if len(rest) > 1:
-        third = {j: block(packed, sweep + 2, j - 1) for j in (1, 2)}
-        apply_blocks(tiles, starts[sweep + 2], third)
-        rest[0][...] = own[:HALF, :]
+def lower(groups, sent, fresh, vectors, front, back, packed, *rest):
+    rest = list(rest)
+    received = None if fresh else rest.pop(0)
+    own = rest.pop(0)
+    message = None if sent is None else rest.pop(0)
+    below = None if fresh else rest.pop(0)
+    if fresh:
+        own[...] = vectors[...]
+    else:
+        below[...] = received[...]
+    apply_groups(tiles_of(own, below=below), groups, front, back)
+    if sent is not None:
+        send_down(own, message, packed, sent)
+
+
+def upper(groups, send, fresh, vectors, front, back, *rest):
+    rest = list(rest)
+    received = None if fresh else rest.pop(0)
+    own = rest.pop(0)
+    message = rest.pop(0) if send else None
+    above = None if fresh else rest.pop(0)
+    if not fresh:
+        above[...] = received[:BAND, :]
+    apply_groups(tiles_of(own, above=above), groups, front, back)
+    if send:
+        message[...] = own[:HALF, :]
 
 
 OWN = (ROWS, COLS)
 UP = (HALF, COLS)
-DOWN = (BAND + 2 * KREF * BAND // COLS, COLS)
-
-
-def step(kernel, name, message, scratch, starts, packed, vectors, *received):
+
+
+def step(kernel, message, scratch, alias, *operands):
     out = [OWN] + ([message] if message else [])
     return pl.pallas_call(
         kernel,
         out_shape=[jax.ShapeDtypeStruct(s, F32) for s in out],
-        in_specs=[SMEM] + [VMEM] * (2 + len(received)),
+        in_specs=[VMEM] * len(operands),
         out_specs=[VMEM] * len(out),
         scratch_shapes=[pltpu.VMEM(s, F32) for s in scratch],
-        input_output_aliases={2: 0},
-        compiler_params=PARAMS,
-        name=name,
-    )(starts, packed, vectors, *received)
+        input_output_aliases={0: 0} if alias else {},
+        compiler_params=PARAMS,
+    )(*operands)
 
 
 def project_kernel(panel, vectors, partial):
@@ -267,23 +303,43 @@
     packed = lax.all_to_all(copies, "col", split_axis=0, concat_axis=0, tiled=True)
     sweeps = mine * lax.axis_size("col")
     fixed = (sweep_start, packed)
-    vectors, downward = step(first_lower, "first_lower", DOWN, (), *fixed, eigvecs)
-    from_above = shifted(downward, 1)
-    vectors, upward = step(first_upper, "first_upper", UP, (), *fixed, vectors)
+    low = [(0, {3: 2})]
+    high = [(0, {1: 0, 2: 1})]
+    ahead = 4
+    ready = prepare(low, *fixed)
+    also = prepare(high, *fixed)
+    kernel = functools.partial(lower, low, range(ahead), True)
+    message = (down_rows(ahead), COLS)
+    vectors, downward = step(kernel, message, (), False, eigvecs, *ready, packed)
+    from_above = edges = shifted(downward, 1)
+    kernel = functools.partial(upper, high, True, True)
+    vectors, upward = step(kernel, UP, (), True, vectors, *also)
     from_below = shifted(upward, -1)
-    for sweep in range(0, sweeps - 2, 2):
-        kernel = functools.partial(lower, sweep)
-        vectors, downward = step(kernel, "lower", DOWN, (UP,), *fixed, vectors, from_below)
-        later = shifted(downward, 1)
-        kernel = functools.partial(upper, sweep)
-        above = (BAND, COLS)
-        vectors, upward = step(kernel, "upper", UP, (above,), *fixed, vectors, from_above)
-        from_below = shifted(upward, -1)
-        from_above = later
-    kernel = functools.partial(lower, sweeps - 2)
-    (vectors,) = step(kernel, "last_lower", None, (UP,), *fixed, vectors, from_below)
-    kernel = functools.partial(upper, sweeps - 2)
-    (vectors,) = step(kernel, "last_upper", None, ((BAND, COLS),), *fixed, vectors, from_above)
+    for sweep in range(0, sweeps, 2):
+        more = sweep + 2 < sweeps
+        place = 2 if sweep == 2 else 0
+        low = [(sweep, {4: 3}), (sweep + 1, {2: 1, 3: 2, 4: 3})]
+        high = [(sweep, {0: place}), (sweep + 1, {0: place + 1, 1: 0})]
+        if more:
+            low.append((sweep + 2, {3: 2}))
+            high.append((sweep + 2, {1: 0, 2: 1}))
+        ready = prepare(low, *fixed)
+        also = prepare(high, *fixed, edges)
+        sent = [k for k in (sweep + ahead, sweep + ahead + 1) if k < sweeps] if more else None
+        kernel = functools.partial(lower, low, sent, False)
+        message = (down_rows(len(sent)), COLS) if more else None
+        done = step(kernel, message, (UP,), True, vectors, *ready, packed, from_below)
+        vectors = done[0]
+        if more:
+            later = shifted(done[1], 1)
+        kernel = functools.partial(upper, high, more, False)
+        message = UP if more else None
+        done = step(kernel, message, ((BAND, COLS),), True, vectors, *also, from_above)
+        vectors = done[0]
+        if more:
+            from_below = shifted(done[1], -1)
+            edges = edges if sweep == 0 else from_above
+            from_above = later
     return final(vectors, panel, row_sum(project(panel, vectors)))
 
 

time: 162 us -> 157 us (0.969)
  waiting for transfers between devices: 41.8 us -> 34.7 us
  starting transfers between devices: 32.6 us -> 34.4 us
    pallas_call x10, Pallas kernels: 22.2 us -> 11.9 us  [step(): pl.pallas_call(kernel, out_shape=[jax.ShapeDtypeStruct(s, F32) for s in o...]
    pallas_call x0 -> x10, Pallas kernels: none -> 10.3 us  [prepare(): pl.pallas_call(functools.partial(prepare_kernel, groups), out_shape=[shap...]
    ppermute x8, waiting for transfers between devices: 38.3 us -> 31.2 us  [shifted(): lax.ppermute(value, 'row', [(k, k + steps) for k in range(begin, end)])]
    ppermute x3, starting transfers between devices: 9.67 us -> 11.5 us  [swapped(): lax.ppermute(value, 'row', [(k, k ^ bit) for k in range(lax.axis_size('ro...]
  transfers between devices with their start and end apart: 11 -> 11, of which waited for: 7 -> 7; matrix products, arithmetic and copies ran while one was open for 0% -> 0% of each run, Pallas kernels for 12% -> 13%
where the time goes in v3:
time: 157 us; the launch traced here: 156 us
  blocking collectives  57 us (36%)
  waiting for transfers between devices  34.7 us (22%)
  starting transfers between devices  34.4 us (22%)
  Pallas kernels  27.1 us (17%)
  local copies, waits for them, and re-layouts  2.62 us (2%)
    ppermute x8, waiting for transfers between devices, shifted(): lax.ppermute(value, 'row', [(k, k + steps) for k in range(begin, end)])  31.2 us
    all_to_all x1, blocking collectives, body(): lax.all_to_all(copies, 'col', split_axis=0, concat_axis=0, tiled=True)  31.2 us
    all_to_all x2, blocking collectives, spread(): lax.all_to_all(value, 'row', split_axis=0, concat_axis=0, tiled=True, axi...  25.8 us
    ppermute x8, starting transfers between devices, shifted(): lax.ppermute(value, 'row', [(k, k + steps) for k in range(begin, end)])  22.9 us
    pallas_call x10, Pallas kernels, step(): pl.pallas_call(kernel, out_shape=[jax.ShapeDtypeStruct(s, F32) for s in o...  11.9 us
    ppermute x3, starting transfers between devices, swapped(): lax.ppermute(value, 'row', [(k, k ^ bit) for k in range(lax.axis_size('ro...  11.5 us
    pallas_call x10, Pallas kernels, prepare(): pl.pallas_call(functools.partial(prepare_kernel, groups), out_shape=[shap...  10.3 us
    ppermute x3, waiting for transfers between devices, swapped(): lax.ppermute(value, 'row', [(k, k ^ bit) for k in range(lax.axis_size('ro...  3.47 us
  transfers between devices with their start and end apart: 11, of which 7 were waited for; matrix products, arithmetic and copies ran while one was open for 0% of the time, Pallas kernels for 13%

profile of v3, /device:TPU:1, one launch (start us, length us, event | category | flops | bytes accessed | tf_op | source)
XLA Modules:
  0.0 156.2 jit_solution(18279882518021439480)
XLA Ops:
  0.9 1.2 copy.17.reflect
  3.0 31.2 %all_to_all.15.packed = f32[4,2,4,64,128]{4,3,2,1,0:T(8,128)S(1)} all-to-all(f32[4,2,4,64,128]{4,3,2,1,0:T(8,128)S(1)} %broadcast_in_dim.6), channel_id=1, replica_groups=mesh['row'=64,'col'=4] {'col'}, dimensions={0} | all-to-all | bytes 2097152 | tf_op jit(solution)/shard_map/all_to_all | solution.py:303
  35.9 7.8 %collective-permute-start.1 = (f32[192,512]{1,0:T(8,128)S(1)}, f32[192,512]{1,0:T(8,128)S(1)}, u32[]{:S(2)}, u32[]{:S(2)}) collective-permute-start(f32[192,512]{1,0:T(8,128)S(1)} %get-tuple-element.51), channel_id=1, source_target_pairs={{0,4},{4,8},{8,12},{12,16},{16,20},{20,24},{24,28},{28,32},{32,36}... | collective-permute-start | bytes 1179656 | tf_op jit(solution)/shard_map/ppermute | solution.py:264
  45.2 1.9 %collective-permute-start = (f32[64,512]{1,0:T(8,128)S(1)}, f32[64,512]{1,0:T(8,128)S(1)}, u32[]{:S(2)}, u32[]{:S(2)}) collective-permute-start(f32[64,512]{1,0:T(8,128)S(1)} %get-tuple-element.49), channel_id=1, source_target_pairs={{4,0},{8,4},{12,8},{16,12},{20,16},{24,20},{28,24},{32,28},{36,32}... | collective-permute-start | bytes 393224 | tf_op jit(solution)/shard_map/ppermute | solution.py:264
  47.1 1.1 prepare.12
  48.2 8.5 %collective-permute-done.rest_0_ = f32[64,512]{1,0:T(8,128)S(1)} collective-permute-done((f32[64,512]{1,0:T(8,128)S(1)}, f32[64,512]{1,0:T(8,128)S(1)}, u32[]{:S(2)}, u32[]{:S(2)}) %collective-permute-start) | collective-permute-done | bytes 131104 | tf_op jit(solution)/shard_map/ppermute | solution.py:264
  56.7 1.4 shard_map.66
  58.1 1.9 %collective-permute-start.3 = (f32[160,512]{1,0:T(8,128)S(1)}, f32[160,512]{1,0:T(8,128)S(1)}, u32[]{:S(2)}, u32[]{:S(2)}) collective-permute-start(f32[160,512]{1,0:T(8,128)S(1)} %get-tuple-element.61), channel_id=1, source_target_pairs={{0,4},{4,8},{8,12},{12,16},{16,20},{20,24},{24,28},{28,32},{32,36}... | collective-permute-start | bytes 983048 | tf_op jit(solution)/shard_map/ppermute | solution.py:264
  60.1 1.1 prepare.13
  61.1 1.5 shard_map.67
  62.7 2.4 %collective-permute-start.2 = (f32[64,512]{1,0:T(8,128)S(1)}, f32[64,512]{1,0:T(8,128)S(1)}, u32[]{:S(2)}, u32[]{:S(2)}) collective-permute-start(f32[64,512]{1,0:T(8,128)S(1)} %get-tuple-element.57), channel_id=1, source_target_pairs={{4,0},{8,4},{12,8},{16,12},{20,16},{24,20},{28,24},{32,28},{36,32}... | collective-permute-start | bytes 393224 | tf_op jit(solution)/shard_map/ppermute | solution.py:264
  65.1 1.1 prepare.14
  66.2 8.4 %collective-permute-done.2.rest_0_ = f32[64,512]{1,0:T(8,128)S(1)} collective-permute-done((f32[64,512]{1,0:T(8,128)S(1)}, f32[64,512]{1,0:T(8,128)S(1)}, u32[]{:S(2)}, u32[]{:S(2)}) %collective-permute-start.2) | collective-permute-done | bytes 131104 | tf_op jit(solution)/shard_map/ppermute | solution.py:264
  74.6 1.4 shard_map.68
  76.0 1.9 %collective-permute-start.5 = (f32[160,512]{1,0:T(8,128)S(1)}, f32[160,512]{1,0:T(8,128)S(1)}, u32[]{:S(2)}, u32[]{:S(2)}) collective-permute-start(f32[160,512]{1,0:T(8,128)S(1)} %get-tuple-element.69), channel_id=1, source_target_pairs={{0,4},{4,8},{8,12},{12,16},{16,20},{20,24},{24,28},{28,32},{32,36}... | collective-permute-start | bytes 983048 | tf_op jit(solution)/shard_map/ppermute | solution.py:264
  78.0 1.1 prepare.15
  79.0 1.5 shard_map.69
  80.6 2.4 %collective-permute-start.4 = (f32[64,512]{1,0:T(8,128)S(1)}, f32[64,512]{1,0:T(8,128)S(1)}, u32[]{:S(2)}, u32[]{:S(2)}) collective-permute-start(f32[64,512]{1,0:T(8,128)S(1)} %get-tuple-element.65), channel_id=1, source_target_pairs={{4,0},{8,4},{12,8},{16,12},{20,16},{24,20},{28,24},{32,28},{36,32}... | collective-permute-start | bytes 393224 | tf_op jit(solution)/shard_map/ppermute | solution.py:264
  83.0 1.1 prepare.16
  84.1 8.4 %collective-permute-done.4.rest_0_ = f32[64,512]{1,0:T(8,128)S(1)} collective-permute-done((f32[64,512]{1,0:T(8,128)S(1)}, f32[64,512]{1,0:T(8,128)S(1)}, u32[]{:S(2)}, u32[]{:S(2)}) %collective-permute-start.4) | collective-permute-done | bytes 131104 | tf_op jit(solution)/shard_map/ppermute | solution.py:264
  92.5 1.4 shard_map.70
  93.9 1.9 %collective-permute-start.7 = (f32[128,512]{1,0:T(8,128)S(1)}, f32[128,512]{1,0:T(8,128)S(1)}, u32[]{:S(2)}, u32[]{:S(2)}) collective-permute-start(f32[128,512]{1,0:T(8,128)S(1)} %get-tuple-element.76), channel_id=1, source_target_pairs={{0,4},{4,8},{8,12},{12,16},{16,20},{20,24},{24,28},{28,32},{32,36}... | collective-permute-start | bytes 786440 | tf_op jit(solution)/shard_map/ppermute | solution.py:264
  95.9 1.1 prepare.17
  96.9 1.5 shard_map.71
  98.5 2.6 %collective-permute-start.6 = (f32[64,512]{1,0:T(8,128)S(1)}, f32[64,512]{1,0:T(8,128)S(1)}, u32[]{:S(2)}, u32[]{:S(2)}) collective-permute-start(f32[64,512]{1,0:T(8,128)S(1)} %get-tuple-element.73), channel_id=1, source_target_pairs={{4,0},{8,4},{12,8},{16,12},{20,16},{24,20},{28,24},{32,28},{36,32}... | collective-permute-start | bytes 393224 | tf_op jit(solution)/shard_map/ppermute | solution.py:264
  103.1 5.9 %collective-permute-done.6.rest_0_ = f32[64,512]{1,0:T(8,128)S(1)} collective-permute-done((f32[64,512]{1,0:T(8,128)S(1)}, f32[64,512]{1,0:T(8,128)S(1)}, u32[]{:S(2)}, u32[]{:S(2)}) %collective-permute-start.6) | collective-permute-done | bytes 131104 | tf_op jit(solution)/shard_map/ppermute | solution.py:264
  111.9 1.4 collective-permute-done.8
  113.3 15.6 %all_to_all.16 = f32[16,4,640]{2,1,0:T(4,128)S(1)} all-to-all(f32[16,4,640]{2,1,0:T(4,128)S(1)} %reshape.6), channel_id=1, replica_groups={{0,16,32,48,64,80,96,112,128,144,160,176,192,208,224,240},{4,20,36,52,6..., dimensions={0} | all-to-all | bytes 327680 | tf_op jit(solution)/shard_map/all_to_all | solution.py:272
  129.0 7.7 %collective-permute-start.9 = (f32[4,640]{1,0:T(4,128)S(1)}, f32[4,640]{1,0:T(4,128)S(1)}, u32[]{:S(2)}, u32[]{:S(2)}) collective-permute-start(f32[4,640]{1,0:T(4,128)S(1)} %reduce_sum.9), channel_id=1, source_target_pairs={{0,8},{4,12},{8,0},{12,4},{16,24},{20,28},{24,16},{28,20},{32,40},... | collective-permute-start | bytes 30728 | tf_op jit(solution)/shard_map/ppermute | solution.py:268
  137.8 10.2 %all_to_all.17 = f32[16,4,640]{2,1,0:T(4,128)S(1)} all-to-all(f32[16,4,640]{2,1,0:T(4,128)S(1)} %broadcast_in_dim.7), channel_id=1, replica_groups={{0,16,32,48,64,80,96,112,128,144,160,176,192,208,224,240},{4,20,36,52,6..., dimensions={0} | all-to-all | bytes 327680 | tf_op jit(solution)/shard_map/all_to_all | solution.py:272
  148.1 3.7 %collective-permute-start.10 = (f32[64,640]{1,0:T(8,128)S(1)}, f32[64,640]{1,0:T(8,128)S(1)}, u32[]{:S(2)}, u32[]{:S(2)}) collective-permute-start(f32[64,640]{1,0:T(8,128)S(1)} %reshape.7), channel_id=1, source_target_pairs={{0,4},{4,0},{8,12},{12,8},{16,20},{20,16},{24,28},{28,24},{32,36},... | collective-permute-start | bytes 491528 | tf_op jit(solution)/shard_map/ppermute | solution.py:268
  152.9 3.3 %final.1 = f32[512,512]{1,0:T(8,128)} custom-call(f32[512,512]{1,0:T(8,128)S(1)} %shard_map.73.vectors, f32[512,128]{1,0:T(8,128)S(1)} %copy-done.2, f32[128,640]{1,0:T(8,128)S(1)} %pad_maximum_fusion.total), custom_call_target="tpu_custom_call" | custom-call | tf_op jit(solution)/shard_map/final/pallas_call | solution.py:251
  (39 shorter events, 12.2 us)
Async XLA Ops:
  0.0 0.7 copy-start
  0.9 1.2 copy-start.3
  3.0 31.2 %copy-start.4 = (s32[8]{0:T(128)S(1)}, s32[8]{0:T(128)}, u32[]{:S(2)}) copy-start(s32[8]{0:T(128)} %starts.19) | copy-start | bytes 100
  34.2 1.2 copy-start.1
  35.9 24.2 %collective-permute-start.1 = (f32[192,512]{1,0:T(8,128)S(1)}, f32[192,512]{1,0:T(8,128)S(1)}, u32[]{:S(2)}, u32[]{:S(2)}) collective-permute-start(f32[192,512]{1,0:T(8,128)S(1)} %get-tuple-element.51), channel_id=1, source_target_pairs={{0,4},{4,8},{8,12},{12,16},{16,20},{20,24},{24,28},{28,32},{32,36}... | collective-permute-start | bytes 1179656 | tf_op jit(solution)/shard_map/ppermute | solution.py:264
  45.2 11.5 %collective-permute-start = (f32[64,512]{1,0:T(8,128)S(1)}, f32[64,512]{1,0:T(8,128)S(1)}, u32[]{:S(2)}, u32[]{:S(2)}) collective-permute-start(f32[64,512]{1,0:T(8,128)S(1)} %get-tuple-element.49), channel_id=1, source_target_pairs={{4,0},{8,4},{12,8},{16,12},{20,16},{24,20},{28,24},{32,28},{36,32}... | collective-permute-start | bytes 393224 | tf_op jit(solution)/shard_map/ppermute | solution.py:264
  58.1 20.9 %collective-permute-start.3 = (f32[160,512]{1,0:T(8,128)S(1)}, f32[160,512]{1,0:T(8,128)S(1)}, u32[]{:S(2)}, u32[]{:S(2)}) collective-permute-start(f32[160,512]{1,0:T(8,128)S(1)} %get-tuple-element.61), channel_id=1, source_target_pairs={{0,4},{4,8},{8,12},{12,16},{16,20},{20,24},{24,28},{28,32},{32,36}... | collective-permute-start | bytes 983048 | tf_op jit(solution)/shard_map/ppermute | solution.py:264
  62.7 11.9 %collective-permute-start.2 = (f32[64,512]{1,0:T(8,128)S(1)}, f32[64,512]{1,0:T(8,128)S(1)}, u32[]{:S(2)}, u32[]{:S(2)}) collective-permute-start(f32[64,512]{1,0:T(8,128)S(1)} %get-tuple-element.57), channel_id=1, source_target_pairs={{4,0},{8,4},{12,8},{16,12},{20,16},{24,20},{28,24},{32,28},{36,32}... | collective-permute-start | bytes 393224 | tf_op jit(solution)/shard_map/ppermute | solution.py:264
  76.0 20.9 %collective-permute-start.5 = (f32[160,512]{1,0:T(8,128)S(1)}, f32[160,512]{1,0:T(8,128)S(1)}, u32[]{:S(2)}, u32[]{:S(2)}) collective-permute-start(f32[160,512]{1,0:T(8,128)S(1)} %get-tuple-element.69), channel_id=1, source_target_pairs={{0,4},{4,8},{8,12},{12,16},{16,20},{20,24},{24,28},{28,32},{32,36}... | collective-permute-start | bytes 983048 | tf_op jit(solution)/shard_map/ppermute | solution.py:264
  80.6 11.9 %collective-permute-start.4 = (f32[64,512]{1,0:T(8,128)S(1)}, f32[64,512]{1,0:T(8,128)S(1)}, u32[]{:S(2)}, u32[]{:S(2)}) collective-permute-start(f32[64,512]{1,0:T(8,128)S(1)} %get-tuple-element.65), channel_id=1, source_target_pairs={{4,0},{8,4},{12,8},{16,12},{20,16},{24,20},{28,24},{32,28},{36,32}... | collective-permute-start | bytes 393224 | tf_op jit(solution)/shard_map/ppermute | solution.py:264
  93.9 16.1 %collective-permute-start.7 = (f32[128,512]{1,0:T(8,128)S(1)}, f32[128,512]{1,0:T(8,128)S(1)}, u32[]{:S(2)}, u32[]{:S(2)}) collective-permute-start(f32[128,512]{1,0:T(8,128)S(1)} %get-tuple-element.76), channel_id=1, source_target_pairs={{0,4},{4,8},{8,12},{12,16},{16,20},{20,24},{24,28},{28,32},{32,36}... | collective-permute-start | bytes 786440 | tf_op jit(solution)/shard_map/ppermute | solution.py:264
  98.5 10.5 %collective-permute-start.6 = (f32[64,512]{1,0:T(8,128)S(1)}, f32[64,512]{1,0:T(8,128)S(1)}, u32[]{:S(2)}, u32[]{:S(2)}) collective-permute-start(f32[64,512]{1,0:T(8,128)S(1)} %get-tuple-element.73), channel_id=1, source_target_pairs={{4,0},{8,4},{12,8},{16,12},{20,16},{24,20},{28,24},{32,28},{36,32}... | collective-permute-start | bytes 393224 | tf_op jit(solution)/shard_map/ppermute | solution.py:264
  110.0 1.0 copy-start.2
  111.8 1.5 collective-permute-start.8
  129.0 8.8 %collective-permute-start.9 = (f32[4,640]{1,0:T(4,128)S(1)}, f32[4,640]{1,0:T(4,128)S(1)}, u32[]{:S(2)}, u32[]{:S(2)}) collective-permute-start(f32[4,640]{1,0:T(4,128)S(1)} %reduce_sum.9), channel_id=1, source_target_pairs={{0,8},{4,12},{8,0},{12,4},{16,24},{20,28},{24,16},{28,20},{32,40},... | collective-permute-start | bytes 30728 | tf_op jit(solution)/shard_map/ppermute | solution.py:268
  148.1 4.7 %collective-permute-start.10 = (f32[64,640]{1,0:T(8,128)S(1)}, f32[64,640]{1,0:T(8,128)S(1)}, u32[]{:S(2)}, u32[]{:S(2)}) collective-permute-start(f32[64,640]{1,0:T(8,128)S(1)} %reshape.7), channel_id=1, source_target_pairs={{0,4},{4,0},{8,12},{12,8},{16,20},{20,16},{24,28},{28,24},{32,36},... | collective-permute-start | bytes 491528 | tf_op jit(solution)/shard_map/ppermute | solution.py:268
